TPU v7x, 768 devices: a whole 4x8x12 slice. The times are simulated.
768 devices in a mesh: dp: 48 (over z, x_hi, core), tensor: 16 (over y, x_lo).
Axes of the slice: x: 4 (x_hi: 2, x_lo: 2; x = x_hi * 2 + x_lo), y: 8, z: 12, core: 2. Of those that a mesh axis runs over, the one named last changes fastest.
Arguments:
- grads: bfloat16 [48, 384, 28672], P('dp', None, 'tensor'), may hold values from -900 to 900
- params: float32 [384, 28672], P('dp', 'tensor'), may hold values from -6 to 6
- moment: float32 [384, 28672], P('dp', 'tensor'), may hold values from -0.6 to 0.6
- variance: float32 [384, 28672], P('dp', 'tensor'), may hold values from 0.01 to 1
- save_owner: int32 [48, 16], P('dp'), may hold values from 0 to 15, each once within a row
Outputs:
- fresh_params: float32 [384, 28672], P('dp', 'tensor')
- moment_next: float32 [384, 28672], P('dp', 'tensor')
- variance_next: float32 [384, 28672], P('dp', 'tensor')
- save_groups: bfloat16 [6144, 1792], P(('dp', 'tensor'))
Inputs may be any that keep to these rules, and one draw needn't show every extreme that they name: Each row of save_owner names every index of 0 to 15 once.
All inputs are finite; a program needn't handle non-finite values.
Results may differ from a plain program's by a relative error of at most 0.001.
Values may be sent and summed in bfloat16 or wider, within the bound.
No kernel may reach another device: no remote copies, remote signals or barrier semaphores. Data moves between devices by JAX's collectives and lax.ppermute only.
A program may use at most 32 MiB of HBM per device.

v0:
```python
import functools
import math

import jax
import jax.numpy as jnp
from jax import lax
from jax.sharding import Mesh
from jax.sharding import PartitionSpec as P

TENSOR = ("tensor_0", "tensor_1")
DP = ("dp_0", "dp_1", "dp_2")
DP_TENSOR = ("dp_0", "dp_1", "dp_2", "tensor_0", "tensor_1")


learn_rate = 0.05
beta_first = 0.9
beta_second = 0.999
adam_step = 1000.0
adam_eps = 1e-08
norm_eps = 1e-06


def one_axis_at_a_time(shard, axes):
    return functools.reduce(lax.psum, axes, shard)


def adam_update(summed, params, moment, variance, clip_scale):
    scaled = clip_scale * summed
    moment_next = beta_first * moment + (1.0 - beta_first) * scaled
    variance_next = beta_second * variance + (1.0 - beta_second) * scaled * scaled
    first_fix = 1.0 - beta_first**adam_step
    second_fix = 1.0 - beta_second**adam_step
    update = moment_next / first_fix / (jnp.sqrt(variance_next / second_fix) + adam_eps)
    return (params - learn_rate * update, moment_next, variance_next)


def add_up(stacked):
    return jnp.sum(stacked, axis=0, dtype=jnp.float32)


def shards(grads, params, moment, variance, save_owner):
    replica_grads = grads[0]
    own_rows = params.shape[0]
    piece_width = params.shape[1]
    tensor_count = lax.axis_size(TENSOR)
    replica_count = lax.axis_size(DP)
    stacked = replica_grads.reshape(replica_count, own_rows, piece_width)
    summed = add_up(lax.all_to_all(stacked, DP, split_axis=0, concat_axis=0, tiled=True))
    squares = one_axis_at_a_time(jnp.sum(summed * summed), DP_TENSOR)
    entries = replica_grads.shape[0] * piece_width * tensor_count
    norm_limit = math.sqrt(float(entries))
    clip_scale = jnp.minimum(1.0, norm_limit / (jnp.sqrt(squares) + norm_eps))
    fresh_params, moment_next, variance_next = adam_update(
        summed, params, moment, variance, clip_scale
    )
    saved_rows = fresh_params.astype(jnp.bfloat16)
    inverse = jnp.argsort(save_owner[0])
    tensor_place = lax.axis_index(TENSOR)
    per_peer = -(-own_rows // tensor_count)
    turn_ids = jnp.arange(per_peer, dtype=jnp.int32)[None, :]
    first_entry = inverse[:, None] * own_rows
    offset = (tensor_place - first_entry) % tensor_count + turn_ids * tensor_count
    usable = offset < own_rows
    source_row = jnp.where(usable, (first_entry + offset) // tensor_count, 0)
    pieces = jnp.take(saved_rows, source_row.reshape(-1), axis=0).reshape(
        tensor_count, per_peer, piece_width
    )
    pieces = jnp.where(usable[:, :, None], pieces, jnp.zeros_like(pieces))
    received = lax.all_to_all(pieces, TENSOR, split_axis=0, concat_axis=0, tiled=True)
    own_start = inverse[tensor_place] * own_rows
    position = jnp.arange(own_rows, dtype=jnp.int32)
    sender = (own_start + position) % tensor_count
    turn_row = position // tensor_count
    flat_received = received.reshape(tensor_count * per_peer, piece_width)
    groups = jnp.take(flat_received, sender * per_peer + turn_row, axis=0)
    return (fresh_params, moment_next, variance_next, groups)


def solution(mesh):
    torus = Mesh(
        mesh.devices.reshape(12, 2, 2, 8, 2), ("dp_0", "dp_1", "dp_2", "tensor_0", "tensor_1")
    )
    return jax.shard_map(
        shards,
        mesh=torus,
        in_specs=(P(DP, None, TENSOR), P(DP, TENSOR), P(DP, TENSOR), P(DP, TENSOR), P(DP, None)),
        out_specs=(P(DP, TENSOR), P(DP, TENSOR), P(DP, TENSOR), P(DP_TENSOR, None)),
        check_vma=False,
    )
```

profile of v0, /device:TPU:2, one launch (start us, length us, event | category | flops | bytes accessed | tf_op | source)
XLA Modules:
  0.0 147.3 jit_solution(17006013027711623390)
XLA Ops:
  0.6 0.0 copy-start.3
  0.6 17.4 %all-to-all-start = ((bf16[48,8,1792]{2,1,0:T(8,128)(2,1)}), bf16[48,8,1792]{2,1,0:T(8,128)(2,1)S(1)}, u32[]{:S(2)}, u32[]{:S(2)}) async-start(bf16[48,8,1792]{2,1,0:T(8,128)(2,1)} %bitcast.13), calls=%async_computation | async-start | bytes 2752512 | tf_op jit(solution)/shard_map/all_to_all | solution.py:48
  18.1 0.0 copy-start
  18.1 0.0 copy-start.1
  18.1 0.0 copy-start.2
  18.1 0.0 copy-done.3
  18.1 1.2 sort.17
  19.4 49.7 %all-to-all-done = bf16[48,8,1792]{2,1,0:T(8,128)(2,1)S(1)} async-done(((bf16[48,8,1792]{2,1,0:T(8,128)(2,1)}), bf16[48,8,1792]{2,1,0:T(8,128)(2,1)S(1)}, u32[]{:S(2)}, u32[]{:S(2)}) %all-to-all-start) | async-done | bytes 1376288 | tf_op jit(solution)/shard_map/all_to_all | solution.py:48
  69.1 0.2 convert_reduce_fusion
  69.3 0.6 multiply_reduce_fusion
  69.9 23.3 %psum.35 = f32[]{:T(128)} all-reduce(f32[]{:T(128)} %multiply_reduce_fusion), channel_id=1, replica_groups=mesh['dp_0'=12,'dp_1'=2,'dp_2'=2,'tensor_0'=8,'tensor_1'=2] {'dp_0'}, use_global_device_ids=true, to_apply=%region_2.0 | all-reduce | flops 1 | bytes 8 | tf_op jit(solution)/shard_map/psum | solution.py:24
  93.3 0.6 dynamic_slice.3
  93.8 7.1 %psum.36 = f32[]{:T(128)} all-reduce(f32[]{:T(128)} %psum.35), channel_id=1, replica_groups=mesh['dp_0'=12,'dp_1'=2,'dp_2'=2,'tensor_0'=8,'tensor_1'=2] {'dp_1'}, use_global_device_ids=true, to_apply=%region_3.0 | all-reduce | flops 1 | bytes 8 | tf_op jit(solution)/shard_map/psum | solution.py:24
  101.5 3.1 %psum.37 = f32[]{:T(128)} all-reduce(f32[]{:T(128)} %psum.36), channel_id=1, replica_groups=mesh['dp_0'=12,'dp_1'=2,'dp_2'=2,'tensor_0'=8,'tensor_1'=2] {'dp_2'}, use_global_device_ids=true, to_apply=%region_4.0 | all-reduce | flops 1 | bytes 8 | tf_op jit(solution)/shard_map/psum | solution.py:24
  104.7 18.3 %psum.38 = f32[]{:T(128)} all-reduce(f32[]{:T(128)} %psum.37), channel_id=1, replica_groups=mesh['dp_0'=12,'dp_1'=2,'dp_2'=2,'tensor_0'=8,'tensor_1'=2] {'tensor_0'}, use_global_device_ids=true, to_apply=%region_5.0 | all-reduce | flops 1 | bytes 8 | tf_op jit(solution)/shard_map/psum | solution.py:24
  122.9 5.6 %psum.39 = f32[]{:T(128)} all-reduce(f32[]{:T(128)} %psum.38), channel_id=1, replica_groups=mesh['dp_0'=12,'dp_1'=2,'dp_2'=2,'tensor_0'=8,'tensor_1'=2] {'tensor_1'}, use_global_device_ids=true, to_apply=%region_6.0 | all-reduce | flops 1 | bytes 8 | tf_op jit(solution)/shard_map/psum | solution.py:24
  129.2 0.0 copy-done
  129.2 0.0 copy-done.1
  129.3 0.0 copy-done.2
  129.3 0.7 fusion.8
  129.9 0.6 gather_fusion
  130.6 0.1 fusion.1
  130.6 0.5 broadcast.286
  131.1 0.7 reduce
  131.8 0.6 reshape.207
  132.5 5.8 %all-to-all-start.1 = ((bf16[16,2,896]{2,1,0:T(2,128)(2,1)}), bf16[16,2,896]{2,1,0:T(2,128)(2,1)S(1)}, u32[]{:S(2)}, u32[]{:S(2)}) async-start(bf16[16,2,896]{2,1,0:T(2,128)(2,1)} %reshape.207), calls=%async_computation.1 | async-start | bytes 114688 | tf_op jit(solution)/shard_map/all_to_all | solution.py:69
  138.3 7.7 %all-to-all-done.1 = bf16[16,2,896]{2,1,0:T(2,128)(2,1)S(1)} async-done(((bf16[16,2,896]{2,1,0:T(2,128)(2,1)}), bf16[16,2,896]{2,1,0:T(2,128)(2,1)S(1)}, u32[]{:S(2)}, u32[]{:S(2)}) %all-to-all-start.1) | async-done | bytes 57376 | tf_op jit(solution)/shard_map/all_to_all | solution.py:69
  146.0 0.6 gather_fusion.1
  146.6 0.7 broadcast_select_fusion
  (9 shorter events, 0.1 us)
Async XLA Ops:
  0.6 17.5 %copy-start.3 = (s32[1,16]{1,0:T(1,128)S(1)}, s32[1,16]{1,0:T(1,128)}, u32[]{:S(2)}) copy-start(s32[1,16]{1,0:T(1,128)} %param.9) | copy-start | bytes 196
  0.6 68.5 %all-to-all-start = ((bf16[48,8,1792]{2,1,0:T(8,128)(2,1)}), bf16[48,8,1792]{2,1,0:T(8,128)(2,1)S(1)}, u32[]{:S(2)}, u32[]{:S(2)}) async-start(bf16[48,8,1792]{2,1,0:T(8,128)(2,1)} %bitcast.13), calls=%async_computation | async-start | bytes 2752512 | tf_op jit(solution)/shard_map/all_to_all | solution.py:48
  18.1 111.2 %copy-start = (f32[8,1792]{1,0:T(8,128)S(1)}, f32[8,1792]{1,0:T(8,128)}, u32[]{:S(2)}) copy-start(f32[8,1792]{1,0:T(8,128)} %param.6) | copy-start | bytes 172036
  18.1 111.2 %copy-start.1 = (f32[8,1792]{1,0:T(8,128)S(1)}, f32[8,1792]{1,0:T(8,128)}, u32[]{:S(2)}) copy-start(f32[8,1792]{1,0:T(8,128)} %param.8) | copy-start | bytes 172036
  18.1 111.2 %copy-start.2 = (f32[8,1792]{1,0:T(8,128)S(1)}, f32[8,1792]{1,0:T(8,128)}, u32[]{:S(2)}) copy-start(f32[8,1792]{1,0:T(8,128)} %param.7) | copy-start | bytes 172036
  132.5 13.5 %all-to-all-start.1 = ((bf16[16,2,896]{2,1,0:T(2,128)(2,1)}), bf16[16,2,896]{2,1,0:T(2,128)(2,1)S(1)}, u32[]{:S(2)}, u32[]{:S(2)}) async-start(bf16[16,2,896]{2,1,0:T(2,128)(2,1)} %reshape.207), calls=%async_computation.1 | async-start | bytes 114688 | tf_op jit(solution)/shard_map/all_to_all | solution.py:69
where the time goes:
time: 148 us; the launch traced here: 147 us
  waiting for transfers between devices  57.4 us (39%)
  blocking collectives  57.3 us (39%)
  starting transfers between devices  23.2 us (16%)
  other arithmetic  4.24 us (3%)
  local copies, waits for them, and re-layouts  2.99 us (2%)
  between operations  2.15 us (1%)
    psum x5, blocking collectives, one_axis_at_a_time(): return functools.reduce(lax.psum, axes, shard)  57.3 us
    all_to_all x1, waiting for transfers between devices, shards(): lax.all_to_all(stacked, DP, split_axis=0, concat_axis=0, tiled=True)  49.7 us
    all_to_all x1, starting transfers between devices, shards(): lax.all_to_all(stacked, DP, split_axis=0, concat_axis=0, tiled=True)  17.4 us
    all_to_all x1, waiting for transfers between devices, shards(): lax.all_to_all(pieces, TENSOR, split_axis=0, concat_axis=0, tiled=True)  7.67 us
    all_to_all x1, starting transfers between devices, shards(): lax.all_to_all(pieces, TENSOR, split_axis=0, concat_axis=0, tiled=True)  5.79 us
  transfers between devices with their start and end apart: 2, of which 2 were waited for; matrix products, arithmetic and copies ran while one was open for 1% of the time, Pallas kernels for 0%

commit v1 on v0

v1 whole, which is shorter than its diff:
```python
import math

import jax
import jax.numpy as jnp
from jax import lax
from jax.sharding import Mesh
from jax.sharding import PartitionSpec as P

TENSOR = ("tensor_0", "tensor_1")
DP = ("dp_0", "dp_1", "dp_2")
DP_TENSOR = ("dp_0", "dp_1", "dp_2", "tensor_0", "tensor_1")
SWAP = ((0, 1), (1, 0))
LANES = 128

learn_rate = 0.05
beta_first = 0.9
beta_second = 0.999
adam_step = 1000.0
adam_eps = 1e-08
norm_eps = 1e-06

SPREAD = 1024.0


def encode(value):
    root = jnp.sqrt(jnp.abs(value)) * SPREAD
    return jnp.where(value < 0.0, -root, root).astype(jnp.float16)


def decode(code):
    root = code.astype(jnp.float32) * (1.0 / SPREAD)
    return root * jnp.abs(root)


def adam_update(summed, params, moment, variance, clip_scale):
    scaled = clip_scale * summed
    moment_next = beta_first * moment + (1.0 - beta_first) * scaled
    variance_next = beta_second * variance + (1.0 - beta_second) * scaled * scaled
    first_fix = 1.0 - beta_first**adam_step
    second_fix = 1.0 - beta_second**adam_step
    update = moment_next / first_fix / (jnp.sqrt(variance_next / second_fix) + adam_eps)
    return (params - learn_rate * update, moment_next, variance_next)


def exchange(array, axes):
    return lax.all_to_all(array, axes, split_axis=0, concat_axis=0, tiled=True)


def total_over(value, axes):
    count = lax.axis_size(axes)
    copies = jnp.broadcast_to(value, (count, 1, LANES))
    return jnp.sum(exchange(copies, axes)[:, 0, 0])


def shards(grads, params, moment, variance, save_owner):
    own_rows, width = params.shape
    tensor_count = lax.axis_size(TENSOR)
    far, core = lax.axis_index("dp_1"), lax.axis_index("dp_2")
    tensor_place = lax.axis_index(TENSOR)
    halves = tensor_count // own_rows
    entries = grads.shape[1] * width * tensor_count
    norm_limit = math.sqrt(float(entries))

    owners = save_owner[0]
    row_owner = jnp.take(owners.reshape(own_rows, halves), tensor_place // own_rows, axis=1)
    slots = jnp.arange(tensor_count, dtype=jnp.int32)
    goes = row_owner[None, :] == slots[:, None]
    source_row = jnp.sum(jnp.where(goes, jnp.arange(own_rows)[None, :], 0), axis=1)
    own_group = jnp.sum(jnp.where(owners == tensor_place, slots, 0))
    first_sender = (own_group % halves) * own_rows

    def pack(array):
        return jnp.take(array, source_row, axis=0)

    def unpack(array):
        return lax.dynamic_slice_in_dim(array, first_sender, own_rows, axis=0)

    state = jnp.stack([params, moment, variance], axis=1)
    state = exchange(pack(state), TENSOR)

    by_place = grads[0].reshape(
        lax.axis_size("dp_0"), lax.axis_size("dp_1"), lax.axis_size("dp_2"), own_rows, width
    )
    kept = lax.dynamic_index_in_dim(by_place, core, axis=2, keepdims=False)
    sent = lax.dynamic_index_in_dim(by_place, 1 - core, axis=2, keepdims=False)
    arrived = lax.ppermute(sent, "dp_2", SWAP)
    pair = kept.astype(jnp.float32) + arrived.astype(jnp.float32)
    kept = lax.dynamic_index_in_dim(pair, far, axis=1, keepdims=False)
    sent = lax.dynamic_index_in_dim(pair, 1 - far, axis=1, keepdims=False)
    four = kept + decode(lax.ppermute(encode(sent), "dp_1", SWAP))
    codes, state = lax.optimization_barrier((encode(four), state))
    state = unpack(state)
    summed = jnp.sum(decode(exchange(codes, "dp_0")), axis=0)

    squares = jnp.sum(summed * summed)
    pieces = jnp.concatenate(
        [pack(summed)[:, None, :], jnp.broadcast_to(squares, (tensor_count, 1, LANES))], axis=2
    )
    received = exchange(pieces, TENSOR)
    group_summed = unpack(received[:, 0, :width])
    squares = jnp.sum(received[:, 0, width])
    squares = total_over(squares, ("dp_1", "dp_2"))
    squares = total_over(squares, "dp_0")
    clip_scale = jnp.minimum(1.0, norm_limit / (jnp.sqrt(squares) + norm_eps))

    fresh_params, moment_next, variance_next = adam_update(
        summed, params, moment, variance, clip_scale
    )
    groups = adam_update(group_summed, state[:, 0], state[:, 1], state[:, 2], clip_scale)[0]
    return (fresh_params, moment_next, variance_next, groups.astype(jnp.bfloat16))


def solution(mesh):
    torus = Mesh(
        mesh.devices.reshape(12, 2, 2, 8, 2), ("dp_0", "dp_1", "dp_2", "tensor_0", "tensor_1")
    )
    return jax.shard_map(
        shards,
        mesh=torus,
        in_specs=(P(DP, None, TENSOR), P(DP, TENSOR), P(DP, TENSOR), P(DP, TENSOR), P(DP, None)),
        out_specs=(P(DP, TENSOR), P(DP, TENSOR), P(DP, TENSOR), P(DP_TENSOR, None)),
        check_vma=False,
    )
```

time: 148 us -> 115 us (0.78)
  the two profiles are of different devices: /device:TPU:2 before, /device:TPU:1 now
where the time goes in v1:
time: 115 us; the launch traced here: 114 us
  starting transfers between devices  35 us (30%)
  waiting for transfers between devices  33.6 us (29%)
  blocking collectives  26.1 us (23%)
  other arithmetic  8.23 us (7%)
  local copies, waits for them, and re-layouts  7.4 us (6%)
  between operations  3.59 us (3%)
    all_to_all x4, waiting for transfers between devices, exchange(): return lax.all_to_all(array, axes, split_axis=0, concat_axis=0, tiled=True)  27 us
    all_to_all x1, blocking collectives, exchange(): return lax.all_to_all(array, axes, split_axis=0, concat_axis=0, tiled=True)  26.1 us
    all_to_all x4, starting transfers between devices, exchange(): return lax.all_to_all(array, axes, split_axis=0, concat_axis=0, tiled=True)  20.7 us
    ppermute x1, starting transfers between devices, shards(): arrived = lax.ppermute(sent, 'dp_2', SWAP)  12.4 us
    ppermute x1, waiting for transfers between devices, shards(): four = kept + decode(lax.ppermute(encode(sent), 'dp_1', SWAP))  6.59 us
    broadcast_in_dim x2, local copies, waits for them, and re-layouts, total_over(): copies = jnp.broadcast_to(value, (count, 1, LANES))  2.46 us
  transfers between devices with their start and end apart: 6, of which 5 were waited for; matrix products, arithmetic and copies ran while one was open for 4% of the time, Pallas kernels for 0%

profile of v1, /device:TPU:1, one launch (start us, length us, event | category | flops | bytes accessed | tf_op | source)
XLA Modules:
  0.0 113.9 jit_solution(5895483309861399992)
XLA Ops:
  0.6 0.0 copy-start.2
  0.6 0.0 copy-start.3
  0.7 0.0 copy-start.1
  0.7 0.0 copy-start.4
  0.7 0.0 copy-start
  0.7 1.3 %dynamic-slice_bitcast_fusion = bf16[12,2,8,1792]{3,2,1,0:T(8,128)(2,1)S(1)} fusion(bf16[12,2,2,8,1792]{4,3,2,1,0:T(8,128)(2,1)} %bitcast.56, s32[]{:T(128)S(6)} %select_n.95), kind=kLoop, calls=%fused_computation.12 | loop fusion | bytes 1376260 | tf_op jit(solution)/shard_map/jit(dynamic_index_in_dim)/squeeze | solution.py:85
  1.9 12.4 %collective-permute-start = (bf16[12,2,8,1792]{3,2,1,0:T(8,128)(2,1)S(1)}, bf16[12,2,8,1792]{3,2,1,0:T(8,128)(2,1)}, u32[]{:S(2)}, u32[]{:S(2)}) collective-permute-start(bf16[12,2,8,1792]{3,2,1,0:T(8,128)(2,1)S(1)} %dynamic-slice_bitcast_fusion), channel_id=1, source_target_pairs={{0,16},{16,0},{1,17},{17,1},{2,18},{18,2},{3,19},{19,3},{4,20},{20... | collective-permute-start | bytes 2064392 | tf_op jit(solution)/shard_map/ppermute | solution.py:86
  14.4 0.0 copy-done.2
  14.4 0.0 copy-done.3
  14.5 0.0 copy-done.1
  14.5 0.5 broadcast.196
  15.1 0.0 copy-done.4
  15.1 0.7 reduce.8
  15.7 0.1 reshape_squeeze.6
  15.8 0.2 select_reduce_fusion
  16.0 0.1 select_reduce_fusion.1
  16.1 0.2 pad_maximum_fusion
  16.3 0.8 gather_fusion
  17.1 0.0 collective-permute-done
  17.1 0.0 copy-done
  17.1 1.3 %convert_add_fusion = f32[12,2,8,1792]{3,2,1,0:T(8,128)S(1)} fusion(bf16[12,2,8,1792]{3,2,1,0:T(8,128)(2,1)} %collective-permute-done, bf16[12,2,2,8,1792]{4,3,2,1,0:T(8,128)(2,1)S(1)} %bitcast.57, s32[]{:T(128)S(6)} %select_n.94), kind=kLoop, calls=%fused_computation.2 | loop fusion | flops 1032192 | bytes 2752516 | tf_op jit(solution)/shard_map/add | solution.py:87
  18.4 0.3 fusion
  18.7 1.9 %collective-permute-start.1 = (f16[12,8,1792]{2,1,0:T(8,128)(2,1)S(1)}, f16[12,8,1792]{2,1,0:T(8,128)(2,1)S(1)}, u32[]{:S(2)}, u32[]{:S(2)}) collective-permute-start(f16[12,8,1792]{2,1,0:T(8,128)(2,1)S(1)} %fusion), channel_id=1, source_target_pairs={{0,32},{32,0},{1,33},{33,1},{2,34},{34,2},{3,35},{35,3},{4,36},{36... | collective-permute-start | bytes 1032200 | tf_op jit(solution)/shard_map/ppermute | solution.py:90
  20.7 0.9 broadcast_select_fusion
  21.6 3.6 %all-to-all-start = ((f32[16,3,1792]{2,1,0:T(4,128)}), f32[16,3,1792]{2,1,0:T(4,128)S(1)}, u32[]{:S(2)}, u32[]{:S(2)}) async-start(f32[16,3,1792]{2,1,0:T(4,128)} %broadcast_select_fusion), calls=%async_computation | async-start | bytes 917504 | tf_op jit(solution)/shard_map/all_to_all | solution.py:46
  25.2 6.6 %collective-permute-done.1 = f16[12,8,1792]{2,1,0:T(8,128)(2,1)S(1)} collective-permute-done((f16[12,8,1792]{2,1,0:T(8,128)(2,1)S(1)}, f16[12,8,1792]{2,1,0:T(8,128)(2,1)S(1)}, u32[]{:S(2)}, u32[]{:S(2)}) %collective-permute-start.1) | collective-permute-done | bytes 344096 | tf_op jit(solution)/shard_map/ppermute | solution.py:90
  31.8 0.4 fusion.2
  32.2 8.2 %all-to-all-done = f32[16,3,1792]{2,1,0:T(4,128)S(1)} async-done(((f32[16,3,1792]{2,1,0:T(4,128)}), f32[16,3,1792]{2,1,0:T(4,128)S(1)}, u32[]{:S(2)}, u32[]{:S(2)}) %all-to-all-start) | async-done | bytes 344096 | tf_op jit(solution)/shard_map/all_to_all | solution.py:46
  40.3 26.1 %all_to_all.25 = f16[12,8,1792]{2,1,0:T(8,128)(2,1)S(1)} all-to-all(f16[12,8,1792]{2,1,0:T(8,128)(2,1)S(1)} %fusion.2), channel_id=1, replica_groups=mesh['dp_0'=12,'dp_1'=2,'dp_2'=2,'tensor_0'=8,'tensor_1'=2] {'dp_0'}, dimensions={0} | all-to-all | bytes 688128 | tf_op jit(solution)/shard_map/all_to_all | solution.py:46
  66.4 0.1 fusion.3
  66.6 0.6 gather_fusion.1
  67.2 0.6 multiply_reduce_fusion
  67.8 0.1 bitcast_select_fusion
  67.9 0.1 copy.37
  68.0 1.4 %concatenate.3.clone = f32[16,1,1920]{2,1,0:T(1,128)} pad(f32[16,1,1792]{2,1,0:T(1,128)S(1)} %copy.37, f32[]{:T(128)} %multiply_reduce_fusion), padding=0_0x0_0x0_128 | pad | bytes 237572 | tf_op jit(solution)/shard_map/concatenate | solution.py:96
  69.4 6.8 %all-to-all-start.2 = ((f32[16,1,1920]{2,1,0:T(1,128)}), f32[16,1,1920]{2,1,0:T(1,128)S(1)}, u32[]{:S(2)}, u32[]{:S(2)}) async-start(f32[16,1,1920]{2,1,0:T(1,128)} %concatenate.3.clone), calls=%async_computation.2 | async-start | bytes 245760 | tf_op jit(solution)/shard_map/all_to_all | solution.py:46
  76.1 0.6 fusion.17
  78.7 5.8 %all-to-all-done.2 = f32[16,1,1920]{2,1,0:T(1,128)S(1)} async-done(((f32[16,1,1920]{2,1,0:T(1,128)}), f32[16,1,1920]{2,1,0:T(1,128)S(1)}, u32[]{:S(2)}, u32[]{:S(2)}) %all-to-all-start.2) | async-done | bytes 122912 | tf_op jit(solution)/shard_map/all_to_all | solution.py:46
  84.5 0.6 slice_reduce_fusion
  85.1 1.2 %broadcast_in_dim.61 = f32[4,1,128]{2,1,0:T(1,128)} broadcast(f32[]{:T(128)} %slice_reduce_fusion), dimensions={} | broadcast | bytes 2052 | tf_op jit(solution)/shard_map/broadcast_in_dim | solution.py:51
  86.4 6.9 %all-to-all-start.3 = ((f32[4,1,128]{2,1,0:T(1,128)}), f32[4,1,128]{2,1,0:T(1,128)S(1)}, u32[]{:S(2)}, u32[]{:S(2)}) async-start(f32[4,1,128]{2,1,0:T(1,128)} %broadcast_in_dim.61), calls=%async_computation.3 | async-start | bytes 4096 | tf_op jit(solution)/shard_map/all_to_all | solution.py:46
  93.3 0.2 constant_dynamic-slice_fusion.1
  93.5 4.3 %all-to-all-done.3 = f32[4,1,128]{2,1,0:T(1,128)S(1)} async-done(((f32[4,1,128]{2,1,0:T(1,128)}), f32[4,1,128]{2,1,0:T(1,128)S(1)}, u32[]{:S(2)}, u32[]{:S(2)}) %all-to-all-start.3) | async-done | bytes 2080 | tf_op jit(solution)/shard_map/all_to_all | solution.py:46
  97.8 0.6 slice_reduce_fusion.2
  98.4 1.2 %broadcast_in_dim.62 = f32[12,1,128]{2,1,0:T(1,128)} broadcast(f32[]{:T(128)} %slice_reduce_fusion.2), dimensions={} | broadcast | bytes 6148 | tf_op jit(solution)/shard_map/broadcast_in_dim | solution.py:51
  99.6 3.5 %all-to-all-start.4 = ((f32[12,1,128]{2,1,0:T(1,128)}), f32[12,1,128]{2,1,0:T(1,128)S(1)}, u32[]{:S(2)}, u32[]{:S(2)}) async-start(f32[12,1,128]{2,1,0:T(1,128)} %broadcast_in_dim.62), calls=%async_computation.4 | async-start | bytes 12288 | tf_op jit(solution)/shard_map/all_to_all | solution.py:46
  103.1 8.8 %all-to-all-done.4 = f32[12,1,128]{2,1,0:T(1,128)S(1)} async-done(((f32[12,1,128]{2,1,0:T(1,128)}), f32[12,1,128]{2,1,0:T(1,128)S(1)}, u32[]{:S(2)}, u32[]{:S(2)}) %all-to-all-start.4) | async-done | bytes 6176 | tf_op jit(solution)/shard_map/all_to_all | solution.py:46
  111.9 0.6 slice_reduce_fusion.1
  113.2 0.7 multiply_subtract_fusion
  (8 shorter events, 0.2 us)
Async XLA Ops:
  0.6 13.7 %copy-start.2 = (f32[8,1792]{1,0:T(8,128)S(1)}, f32[8,1792]{1,0:T(8,128)}, u32[]{:S(2)}) copy-start(f32[8,1792]{1,0:T(8,128)} %param.8) | copy-start | bytes 172036
  0.6 13.8 %copy-start.3 = (f32[8,1792]{1,0:T(8,128)S(1)}, f32[8,1792]{1,0:T(8,128)}, u32[]{:S(2)}) copy-start(f32[8,1792]{1,0:T(8,128)} %param.7) | copy-start | bytes 172036
  0.7 13.8 %copy-start.1 = (f32[8,1792]{1,0:T(8,128)S(1)}, f32[8,1792]{1,0:T(8,128)}, u32[]{:S(2)}) copy-start(f32[8,1792]{1,0:T(8,128)} %param.6) | copy-start | bytes 172036
  0.7 14.4 %copy-start.4 = (s32[1,16]{1,0:T(1,128)S(1)}, s32[1,16]{1,0:T(1,128)}, u32[]{:S(2)}) copy-start(s32[1,16]{1,0:T(1,128)} %param.9) | copy-start | bytes 196
  0.7 16.4 %copy-start = (bf16[1,384,1792]{2,1,0:T(8,128)(2,1)S(1)}, bf16[1,384,1792]{2,1,0:T(8,128)(2,1)}, u32[]{:S(2)}) copy-start(bf16[1,384,1792]{2,1,0:T(8,128)(2,1)} %param.5) | copy-start | bytes 4128772
  1.9 15.2 %collective-permute-start = (bf16[12,2,8,1792]{3,2,1,0:T(8,128)(2,1)S(1)}, bf16[12,2,8,1792]{3,2,1,0:T(8,128)(2,1)}, u32[]{:S(2)}, u32[]{:S(2)}) collective-permute-start(bf16[12,2,8,1792]{3,2,1,0:T(8,128)(2,1)S(1)} %dynamic-slice_bitcast_fusion), channel_id=1, source_target_pairs={{0,16},{16,0},{1,17},{17,1},{2,18},{18,2},{3,19},{19,3},{4,20},{20... | collective-permute-start | bytes 2064392 | tf_op jit(solution)/shard_map/ppermute | solution.py:86
  18.7 13.0 %collective-permute-start.1 = (f16[12,8,1792]{2,1,0:T(8,128)(2,1)S(1)}, f16[12,8,1792]{2,1,0:T(8,128)(2,1)S(1)}, u32[]{:S(2)}, u32[]{:S(2)}) collective-permute-start(f16[12,8,1792]{2,1,0:T(8,128)(2,1)S(1)} %fusion), channel_id=1, source_target_pairs={{0,32},{32,0},{1,33},{33,1},{2,34},{34,2},{3,35},{35,3},{4,36},{36... | collective-permute-start | bytes 1032200 | tf_op jit(solution)/shard_map/ppermute | solution.py:90
  21.6 18.7 %all-to-all-start = ((f32[16,3,1792]{2,1,0:T(4,128)}), f32[16,3,1792]{2,1,0:T(4,128)S(1)}, u32[]{:S(2)}, u32[]{:S(2)}) async-start(f32[16,3,1792]{2,1,0:T(4,128)} %broadcast_select_fusion), calls=%async_computation | async-start | bytes 917504 | tf_op jit(solution)/shard_map/all_to_all | solution.py:46
  69.4 15.2 %all-to-all-start.2 = ((f32[16,1,1920]{2,1,0:T(1,128)}), f32[16,1,1920]{2,1,0:T(1,128)S(1)}, u32[]{:S(2)}, u32[]{:S(2)}) async-start(f32[16,1,1920]{2,1,0:T(1,128)} %concatenate.3.clone), calls=%async_computation.2 | async-start | bytes 245760 | tf_op jit(solution)/shard_map/all_to_all | solution.py:46
  86.4 11.4 %all-to-all-start.3 = ((f32[4,1,128]{2,1,0:T(1,128)}), f32[4,1,128]{2,1,0:T(1,128)S(1)}, u32[]{:S(2)}, u32[]{:S(2)}) async-start(f32[4,1,128]{2,1,0:T(1,128)} %broadcast_in_dim.61), calls=%async_computation.3 | async-start | bytes 4096 | tf_op jit(solution)/shard_map/all_to_all | solution.py:46
  99.6 12.3 %all-to-all-start.4 = ((f32[12,1,128]{2,1,0:T(1,128)}), f32[12,1,128]{2,1,0:T(1,128)S(1)}, u32[]{:S(2)}, u32[]{:S(2)}) async-start(f32[12,1,128]{2,1,0:T(1,128)} %broadcast_in_dim.62), calls=%async_computation.4 | async-start | bytes 12288 | tf_op jit(solution)/shard_map/all_to_all | solution.py:46

commit v2 on v1

v2 whole, which is shorter than its diff:
```python
import functools
import math

import jax
import jax.numpy as jnp
from jax import lax
from jax.experimental import pallas as pl
from jax.experimental.pallas import tpu as pltpu
from jax.sharding import Mesh
from jax.sharding import PartitionSpec as P


TENSOR = ("tensor_0", "tensor_1")
DP = ("dp_0", "dp_1", "dp_2")
DP_TENSOR = ("dp_0", "dp_1", "dp_2", "tensor_0", "tensor_1")
SWAP = ((0, 1), (1, 0))
LANES = 128

learn_rate = 0.05
beta_first = 0.9
beta_second = 0.999
adam_step = 1000.0
adam_eps = 1e-08
norm_eps = 1e-06

SPREAD = 16.0


def encode(value):
    return (value * SPREAD).astype(jnp.float16)


def decode(code):
    return code.astype(jnp.float32) * (1.0 / SPREAD)


def adam_update(summed, params, moment, variance, clip_scale):
    scaled = clip_scale * summed
    moment_next = beta_first * moment + (1.0 - beta_first) * scaled
    variance_next = beta_second * variance + (1.0 - beta_second) * scaled * scaled
    first_fix = 1.0 - beta_first**adam_step
    second_fix = 1.0 - beta_second**adam_step
    update = moment_next / first_fix / (jnp.sqrt(variance_next / second_fix) + adam_eps)
    return (params - learn_rate * update, moment_next, variance_next)


def exchange(array, axes):
    return lax.all_to_all(array, axes, split_axis=0, concat_axis=0, tiled=True)


def in_vmem():
    return pl.BlockSpec(memory_space=pltpu.VMEM)


def keep(array):
    return pltpu.with_memory_space_constraint(array, pltpu.VMEM)


def in_smem():
    return pl.BlockSpec(memory_space=pltpu.SMEM)


def pack_state(owners, params, moment, variance, out):
    own_rows, width = params.shape
    halves = owners.shape[1] // own_rows
    half = lax.axis_index(TENSOR) // own_rows
    for row in range(own_rows):
        slot = owners[0, row * halves + half]
        for place, array in enumerate((params, moment, variance)):
            out[slot, :, place * width : (place + 1) * width] = array[row : row + 1, :]


def pack_summed(owners, summed, out):
    own_rows, width = summed.shape
    halves = owners.shape[1] // own_rows
    half = lax.axis_index(TENSOR) // own_rows
    squares = jnp.zeros((own_rows, LANES), jnp.float32)
    for start in range(0, width, LANES):
        tile = summed[:, start : start + LANES]
        squares = squares + tile * tile
    squares = jnp.sum(squares, axis=0, keepdims=True)
    for slot in range(out.shape[0]):
        out[slot, :, width:] = squares
    for row in range(own_rows):
        slot = owners[0, row * halves + half]
        out[slot, :, :width] = summed[row : row + 1, :]


def finish(norm_limit, owners, squares, received, state, summed, params, moment, variance,
           fresh_out, moment_out, variance_out, groups_out):
    own_rows, width = params.shape
    tensor_count = owners.shape[1]
    halves = tensor_count // own_rows
    place = lax.axis_index(TENSOR)
    first = jnp.int32(0)
    for group in range(tensor_count):
        first = jnp.where(owners[0, group] == place, group % halves * own_rows, first)
    norm = jnp.sqrt(jnp.sum(jnp.sum(squares[...], axis=0), axis=1, keepdims=True))
    clip_scale = jnp.minimum(1.0, norm_limit / (norm + norm_eps))
    fresh, moment_next, variance_next = adam_update(
        summed[...], params[...], moment[...], variance[...], clip_scale
    )
    fresh_out[...] = fresh
    moment_out[...] = moment_next
    variance_out[...] = variance_next

    def rows(array, start):
        return jnp.concatenate(
            [array[first + row, :, start : start + width] for row in range(own_rows)], axis=0
        )

    groups = adam_update(
        rows(received, 0), rows(state, 0), rows(state, width), rows(state, 2 * width), clip_scale
    )[0]
    groups_out[...] = groups.astype(groups_out.dtype)


def shards(grads, params, moment, variance, save_owner):
    own_rows, width = params.shape
    tensor_count = lax.axis_size(TENSOR)
    far, core = lax.axis_index("dp_1"), lax.axis_index("dp_2")
    norm_limit = math.sqrt(float(grads.shape[1] * width * tensor_count))
    tile = jax.ShapeDtypeStruct((own_rows, width), jnp.float32)

    by_place = grads[0].reshape(
        lax.axis_size("dp_0"), lax.axis_size("dp_1"), lax.axis_size("dp_2"), own_rows, width
    )
    kept = lax.dynamic_index_in_dim(by_place, core, axis=2, keepdims=False)
    sent = lax.dynamic_index_in_dim(by_place, 1 - core, axis=2, keepdims=False)
    arrived = lax.ppermute(sent, "dp_2", SWAP)

    def pair_sum(side):
        return lax.dynamic_index_in_dim(kept, side, axis=1, keepdims=False).astype(
            jnp.float32
        ) + lax.dynamic_index_in_dim(arrived, side, axis=1, keepdims=False).astype(jnp.float32)

    params, moment, variance = map(keep, (params, moment, variance))
    state = pl.pallas_call(
        pack_state,
        out_shape=jax.ShapeDtypeStruct((tensor_count, 1, 3 * width), jnp.float32),
        in_specs=[in_smem()] + [in_vmem()] * 3,
        out_specs=in_vmem(),
    )(save_owner, params, moment, variance)
    state = exchange(state, TENSOR)

    code = encode(pair_sum(1 - far))
    code = lax.ppermute(code, "dp_1", SWAP)
    four = pair_sum(far) + decode(code)

    codes, state = lax.optimization_barrier((encode(four), state))
    summed = jnp.sum(decode(exchange(codes, "dp_0")), axis=0)

    pieces = pl.pallas_call(
        pack_summed,
        out_shape=pltpu.VMEM((tensor_count, 1, width + LANES), jnp.float32),
        in_specs=[in_smem(), in_vmem()],
        out_specs=in_vmem(),
    )(save_owner, keep(summed))
    received = exchange(pieces, TENSOR)
    squares = jnp.sum(received[:, :, width:], axis=0, keepdims=True)
    squares = exchange(jnp.broadcast_to(squares, (4, 1, LANES)), ("dp_1", "dp_2"))
    squares = jnp.sum(squares, axis=0, keepdims=True)
    squares = exchange(jnp.broadcast_to(squares, (12, 1, LANES)), "dp_0")

    return pl.pallas_call(
        functools.partial(finish, norm_limit),
        out_shape=(tile, tile, tile, jax.ShapeDtypeStruct(tile.shape, jnp.bfloat16)),
        in_specs=[in_smem()] + [in_vmem()] * 7,
        out_specs=[in_vmem()] * 4,
    )(save_owner, *map(keep, (squares, received, state, summed)), params, moment, variance)


def solution(mesh):
    torus = Mesh(
        mesh.devices.reshape(12, 2, 2, 8, 2), ("dp_0", "dp_1", "dp_2", "tensor_0", "tensor_1")
    )
    return jax.shard_map(
        shards,
        mesh=torus,
        in_specs=(P(DP, None, TENSOR), P(DP, TENSOR), P(DP, TENSOR), P(DP, TENSOR), P(DP, None)),
        out_specs=(P(DP, TENSOR), P(DP, TENSOR), P(DP, TENSOR), P(DP_TENSOR, None)),
        check_vma=False,
    )
```

time: 115 us -> 103 us (0.90)
  blocking collectives: 26.1 us -> 63.7 us
  waiting for transfers between devices: 33.6 us -> 14.3 us
  starting transfers between devices: 35 us -> 17.8 us
  other arithmetic: 8.23 us -> 0.46 us
  local copies, waits for them, and re-layouts: 7.4 us -> 1.28 us
  Pallas kernels: 0 us -> 3.71 us
  between operations: 3.59 us -> 0.76 us
    all_to_all x1 -> x4, blocking collectives: 26.1 us -> 63.7 us  [exchange(): return lax.all_to_all(array, axes, split_axis=0, concat_axis=0, tiled=True)]
    all_to_all x4 -> x1, waiting for transfers between devices: 27 us -> 6.85 us  [exchange(): return lax.all_to_all(array, axes, split_axis=0, concat_axis=0, tiled=True)]
    all_to_all x4 -> x1, starting transfers between devices: 20.7 us -> 3.54 us  [exchange(): return lax.all_to_all(array, axes, split_axis=0, concat_axis=0, tiled=True)]
    pallas_call x0 -> x3, Pallas kernels: none -> 3.71 us  [the longest x1 1.6 us: shards(): pl.pallas_call(functools.partial(finish, norm_limit), out_shape=(tile, ti...]
    reduce_sum x6 -> x2, other arithmetic: 3.16 us -> 0.05 us  [the longest x1 0.03 us: shards(): squares = jnp.sum(received[:, :, width:], axis=0, keepdims=True)]
    broadcast_in_dim x2, local copies, waits for them, and re-layouts: 2.46 us -> 0.01 us  [the longest x1 0.01 us: shards(): squares = exchange(jnp.broadcast_to(squares, (12, 1, LANES)), 'dp_0')]
    ppermute x1, waiting for transfers between devices: 0.01 us -> 1.74 us  [shards(): arrived = lax.ppermute(sent, 'dp_2', SWAP)]
    gather x2 -> x0, local copies, waits for them, and re-layouts: 1.42 us -> none  [pack(): return jnp.take(array, source_row, axis=0)]
  transfers between devices with their start and end apart: 6 -> 3, of which waited for: 5 -> 3; matrix products, arithmetic and copies ran while one was open for 4% -> 0% of each run, Pallas kernels for 0% -> 1%
where the time goes in v2:
time: 103 us; the launch traced here: 102 us
  blocking collectives  63.7 us (62%)
  starting transfers between devices  17.8 us (17%)
  waiting for transfers between devices  14.3 us (14%)
  Pallas kernels  3.71 us (4%)
  local copies, waits for them, and re-layouts  1.28 us (1%)
    all_to_all x4, blocking collectives, exchange(): return lax.all_to_all(array, axes, split_axis=0, concat_axis=0, tiled=True)  63.7 us
    ppermute x1, starting transfers between devices, shards(): arrived = lax.ppermute(sent, 'dp_2', SWAP)  12.4 us
    all_to_all x1, waiting for transfers between devices, exchange(): return lax.all_to_all(array, axes, split_axis=0, concat_axis=0, tiled=True)  6.85 us
    ppermute x1, waiting for transfers between devices, shards(): code = lax.ppermute(code, 'dp_1', SWAP)  5.7 us
    all_to_all x1, starting transfers between devices, exchange(): return lax.all_to_all(array, axes, split_axis=0, concat_axis=0, tiled=True)  3.54 us
  transfers between devices with their start and end apart: 3, of which 3 were waited for; matrix products, arithmetic and copies ran while one was open for 0% of the time, Pallas kernels for 1%

profile of v2, /device:TPU:1, one launch (start us, length us, event | category | flops | bytes accessed | tf_op | source)
XLA Modules:
  0.0 102.1 jit_solution(16061653636807700290)
XLA Ops:
  0.6 0.0 copy-start.3
  0.6 0.0 copy-start
  0.7 0.0 copy-start.1
  0.7 0.0 copy-start.2
  0.7 1.2 %copy_bitcast_fusion = bf16[12,2,8,1792]{3,2,0,1:T(8,128)(2,1)S(1)} fusion(bf16[12,2,2,8,1792]{4,3,2,1,0:T(8,128)(2,1)} %bitcast.18, s32[]{:T(128)S(6)} %select_n.26), kind=kLoop, calls=%fused_computation.7 | loop fusion | bytes 1376260 | tf_op jit(solution)/shard_map/jit(dynamic_index_in_dim)/squeeze | solution.py:129
  1.9 12.4 %collective-permute-start = (bf16[12,2,8,1792]{3,2,0,1:T(8,128)(2,1)S(1)}, bf16[12,2,8,1792]{3,2,0,1:T(8,128)(2,1)S(1)}, u32[]{:S(2)}, u32[]{:S(2)}) collective-permute-start(bf16[12,2,8,1792]{3,2,0,1:T(8,128)(2,1)S(1)} %copy_bitcast_fusion), channel_id=1, source_target_pairs={{0,16},{16,0},{1,17},{17,1},{2,18},{18,2},{3,19},{19,3},{4,20},{20... | collective-permute-start | bytes 2064392 | tf_op jit(solution)/shard_map/ppermute | solution.py:130
  14.3 1.7 %collective-permute-done = bf16[12,2,8,1792]{3,2,0,1:T(8,128)(2,1)S(1)} collective-permute-done((bf16[12,2,8,1792]{3,2,0,1:T(8,128)(2,1)S(1)}, bf16[12,2,8,1792]{3,2,0,1:T(8,128)(2,1)S(1)}, u32[]{:S(2)}, u32[]{:S(2)}) %collective-permute-start) | collective-permute-done | bytes 688160 | tf_op jit(solution)/shard_map/ppermute | solution.py:130
  16.1 0.0 copy-done.3
  16.1 0.1 fusion.1
  16.2 1.9 %collective-permute-start.1 = (f16[12,8,1792]{2,1,0:T(8,128)(2,1)S(1)}, f16[12,8,1792]{2,1,0:T(8,128)(2,1)S(1)}, u32[]{:S(2)}, u32[]{:S(2)}) collective-permute-start(f16[12,8,1792]{2,1,0:T(8,128)(2,1)S(1)} %fusion.1), channel_id=1, source_target_pairs={{0,32},{32,0},{1,33},{33,1},{2,34},{34,2},{3,35},{35,3},{4,36},{36... | collective-permute-start | bytes 1032200 | tf_op jit(solution)/shard_map/ppermute | solution.py:147
  18.1 0.0 copy-done
  18.1 0.0 copy-done.1
  18.2 0.0 copy-done.2
  18.2 1.4 %shard_map.84 = f32[16,1,5376]{2,1,0:T(1,128)} custom-call(s32[1,16]{1,0:T(1,128)} %owners.5, f32[8,1792]{1,0:T(8,128)S(1)} %copy-done, f32[8,1792]{1,0:T(8,128)S(1)} %copy-done.1, f32[8,1792]{1,0:T(8,128)S(1)} %copy-done.2), custom_call_target="tpu_custom_call" | custom-call | tf_op jit(solution)/shard_map/pallas_call | solution.py:138
  19.6 3.5 %all-to-all-start = ((f32[16,1,5376]{2,1,0:T(1,128)}), f32[16,1,5376]{2,1,0:T(1,128)S(1)}, u32[]{:S(2)}, u32[]{:S(2)}) async-start(f32[16,1,5376]{2,1,0:T(1,128)} %shard_map.84), calls=%async_computation | async-start | bytes 688128 | tf_op jit(solution)/shard_map/all_to_all | solution.py:48
  23.1 5.7 %collective-permute-done.1 = f16[12,8,1792]{2,1,0:T(8,128)(2,1)S(1)} collective-permute-done((f16[12,8,1792]{2,1,0:T(8,128)(2,1)S(1)}, f16[12,8,1792]{2,1,0:T(8,128)(2,1)S(1)}, u32[]{:S(2)}, u32[]{:S(2)}) %collective-permute-start.1) | collective-permute-done | bytes 344096 | tf_op jit(solution)/shard_map/ppermute | solution.py:147
  28.8 0.2 fusion.4
  29.1 6.9 %all-to-all-done.state = f32[16,1,5376]{2,1,0:T(1,128)S(1)} async-done(((f32[16,1,5376]{2,1,0:T(1,128)}), f32[16,1,5376]{2,1,0:T(1,128)S(1)}, u32[]{:S(2)}, u32[]{:S(2)}) %all-to-all-start) | async-done | bytes 344096 | tf_op jit(solution)/shard_map/all_to_all | solution.py:48
  35.9 25.9 %all_to_all.25 = f16[12,8,1792]{2,1,0:T(8,128)(2,1)S(1)} all-to-all(f16[12,8,1792]{2,1,0:T(8,128)(2,1)S(1)} %fusion.4), channel_id=1, replica_groups=mesh['dp_0'=12,'dp_1'=2,'dp_2'=2,'tensor_0'=8,'tensor_1'=2] {'dp_0'}, dimensions={0} | all-to-all | bytes 688128 | tf_op jit(solution)/shard_map/all_to_all | solution.py:48
  61.8 0.1 multiply_reduce_fusion.summed
  61.9 0.7 shard_map.85
  62.6 15.1 %all_to_all.26.received = f32[16,1,1920]{2,1,0:T(1,128)S(1)} all-to-all(f32[16,1,1920]{2,1,0:T(1,128)S(1)} %shard_map.85), channel_id=1, replica_groups=mesh['dp_0'=12,'dp_1'=2,'dp_2'=2,'tensor_0'=8,'tensor_1'=2] {'tensor_0',..., dimensions={0} | all-to-all | bytes 245760 | tf_op jit(solution)/shard_map/all_to_all | solution.py:48
  77.8 11.0 %all_to_all.27 = f32[4,1,128]{2,1,0:T(1,128)S(1)} all-to-all(f32[4,1,128]{2,1,0:T(1,128)S(1)} %broadcast_in_dim.4), channel_id=1, replica_groups=mesh['dp_0'=12,'dp_1'=2,'dp_2'=2,'tensor_0'=8,'tensor_1'=2] {'dp_1','dp_2'}, dimensions={0} | all-to-all | bytes 4096 | tf_op jit(solution)/shard_map/all_to_all | solution.py:48
  88.8 11.7 %all_to_all.28.squares = f32[12,1,128]{2,1,0:T(1,128)S(1)} all-to-all(f32[12,1,128]{2,1,0:T(1,128)S(1)} %broadcast_in_dim.5), channel_id=1, replica_groups=mesh['dp_0'=12,'dp_1'=2,'dp_2'=2,'tensor_0'=8,'tensor_1'=2] {'dp_0'}, dimensions={0} | all-to-all | bytes 12288 | tf_op jit(solution)/shard_map/all_to_all | solution.py:48
  100.5 1.6 %shard_map.86 = (f32[8,1792]{1,0:T(8,128)}, f32[8,1792]{1,0:T(8,128)}, f32[8,1792]{1,0:T(8,128)}, bf16[8,1792]{1,0:T(8,128)(2,1)}) custom-call(s32[1,16]{1,0:T(1,128)} %owners.5, f32[12,1,128]{2,1,0:T(1,128)S(1)} %all_to_all.28.squares, f32[16,1,1920]{2,1,0:T(1,128)S(1)} %all_to_all.26.received, f32[16,1,5376]{2,1,0:T(1,128)S(1)} %all-to-all-done.state, ...), custom_call_target="tpu_custom_call" | custom-call | tf_op jit(solution)/shard_map/pallas_call | solution.py:165
  (4 shorter events, 0.1 us)
Async XLA Ops:
  0.6 15.4 %copy-start.3 = (bf16[1,384,1792]{2,1,0:T(8,128)(2,1)S(1)}, bf16[1,384,1792]{2,1,0:T(8,128)(2,1)}, u32[]{:S(2)}) copy-start(bf16[1,384,1792]{2,1,0:T(8,128)(2,1)} %param.5) | copy-start | bytes 4128772
  0.6 17.5 %copy-start = (f32[8,1792]{1,0:T(8,128)S(1)}, f32[8,1792]{1,0:T(8,128)}, u32[]{:S(2)}) copy-start(f32[8,1792]{1,0:T(8,128)} %params.3) | copy-start | bytes 172036
  0.7 17.5 %copy-start.1 = (f32[8,1792]{1,0:T(8,128)S(1)}, f32[8,1792]{1,0:T(8,128)}, u32[]{:S(2)}) copy-start(f32[8,1792]{1,0:T(8,128)} %moment.3) | copy-start | bytes 172036
  0.7 17.5 %copy-start.2 = (f32[8,1792]{1,0:T(8,128)S(1)}, f32[8,1792]{1,0:T(8,128)}, u32[]{:S(2)}) copy-start(f32[8,1792]{1,0:T(8,128)} %variance.3) | copy-start | bytes 172036
  1.9 14.1 %collective-permute-start = (bf16[12,2,8,1792]{3,2,0,1:T(8,128)(2,1)S(1)}, bf16[12,2,8,1792]{3,2,0,1:T(8,128)(2,1)S(1)}, u32[]{:S(2)}, u32[]{:S(2)}) collective-permute-start(bf16[12,2,8,1792]{3,2,0,1:T(8,128)(2,1)S(1)} %copy_bitcast_fusion), channel_id=1, source_target_pairs={{0,16},{16,0},{1,17},{17,1},{2,18},{18,2},{3,19},{19,3},{4,20},{20... | collective-permute-start | bytes 2064392 | tf_op jit(solution)/shard_map/ppermute | solution.py:130
  16.2 12.6 %collective-permute-start.1 = (f16[12,8,1792]{2,1,0:T(8,128)(2,1)S(1)}, f16[12,8,1792]{2,1,0:T(8,128)(2,1)S(1)}, u32[]{:S(2)}, u32[]{:S(2)}) collective-permute-start(f16[12,8,1792]{2,1,0:T(8,128)(2,1)S(1)} %fusion.1), channel_id=1, source_target_pairs={{0,32},{32,0},{1,33},{33,1},{2,34},{34,2},{3,35},{35,3},{4,36},{36... | collective-permute-start | bytes 1032200 | tf_op jit(solution)/shard_map/ppermute | solution.py:147
  19.6 16.3 %all-to-all-start = ((f32[16,1,5376]{2,1,0:T(1,128)}), f32[16,1,5376]{2,1,0:T(1,128)S(1)}, u32[]{:S(2)}, u32[]{:S(2)}) async-start(f32[16,1,5376]{2,1,0:T(1,128)} %shard_map.84), calls=%async_computation | async-start | bytes 688128 | tf_op jit(solution)/shard_map/all_to_all | solution.py:48

commit v3 on v2

--- a/solution.py
+++ b/solution.py
@@ -60,14 +60,34 @@
     return pl.BlockSpec(memory_space=pltpu.SMEM)
 
 
-def pack_state(owners, params, moment, variance, out):
+def load(owners, grads, params, moment, variance, state, kept, sent, *rest):
     own_rows, width = params.shape
     halves = owners.shape[1] // own_rows
     half = lax.axis_index(TENSOR) // own_rows
-    for row in range(own_rows):
-        slot = owners[0, row * halves + half]
-        for place, array in enumerate((params, moment, variance)):
-            out[slot, :, place * width : (place + 1) * width] = array[row : row + 1, :]
+    core = lax.axis_index("dp_2")
+    own, semaphores = rest[:3], rest[3]
+    copies = [
+        pltpu.make_async_copy(array, place, semaphores.at[index])
+        for index, (array, place) in enumerate(zip((params, moment, variance), own))
+    ]
+    for index, (place, whose) in enumerate(((sent, 1 - core), (kept, core))):
+        for side in range(place.shape[0]):
+            copies.append(
+                pltpu.make_async_copy(
+                    grads.at[:, side, whose],
+                    place.at[side],
+                    semaphores.at[3 + index * place.shape[0] + side],
+                )
+            )
+    for copy in copies:
+        copy.start()
+    for place, array in enumerate(own):
+        copies[place].wait()
+        for row in range(own_rows):
+            slot = owners[0, row * halves + half]
+            state[slot, :, place * width : (place + 1) * width] = array[row : row + 1, :]
+    for copy in copies[3:]:
+        copy.wait()
 
 
 def pack_summed(owners, summed, out):
@@ -118,29 +138,35 @@
 def shards(grads, params, moment, variance, save_owner):
     own_rows, width = params.shape
     tensor_count = lax.axis_size(TENSOR)
-    far, core = lax.axis_index("dp_1"), lax.axis_index("dp_2")
+    far = lax.axis_index("dp_1")
     norm_limit = math.sqrt(float(grads.shape[1] * width * tensor_count))
     tile = jax.ShapeDtypeStruct((own_rows, width), jnp.float32)
 
     by_place = grads[0].reshape(
         lax.axis_size("dp_0"), lax.axis_size("dp_1"), lax.axis_size("dp_2"), own_rows, width
     )
-    kept = lax.dynamic_index_in_dim(by_place, core, axis=2, keepdims=False)
-    sent = lax.dynamic_index_in_dim(by_place, 1 - core, axis=2, keepdims=False)
+    core_count = lax.axis_size("dp_2")
+    far_count = lax.axis_size("dp_1")
+    part = pltpu.VMEM((far_count, by_place.shape[0], own_rows, width), grads.dtype)
+    state, kept, sent, params, moment, variance = pl.pallas_call(
+        load,
+        out_shape=(
+            jax.ShapeDtypeStruct((tensor_count, 1, 3 * width), jnp.float32),
+            part,
+            part,
+            *[pltpu.VMEM(tile.shape, tile.dtype)] * 3,
+        ),
+        in_specs=[in_smem()] + [pl.BlockSpec(memory_space=pl.ANY)] * 4,
+        out_specs=[in_vmem()] * 6,
+        scratch_shapes=[pltpu.SemaphoreType.DMA((3 + far_count * core_count,))],
+    )(save_owner, by_place, params, moment, variance)
     arrived = lax.ppermute(sent, "dp_2", SWAP)
 
     def pair_sum(side):
-        return lax.dynamic_index_in_dim(kept, side, axis=1, keepdims=False).astype(
+        return lax.dynamic_index_in_dim(kept, side, axis=0, keepdims=False).astype(
             jnp.float32
-        ) + lax.dynamic_index_in_dim(arrived, side, axis=1, keepdims=False).astype(jnp.float32)
-
-    params, moment, variance = map(keep, (params, moment, variance))
-    state = pl.pallas_call(
-        pack_state,
-        out_shape=jax.ShapeDtypeStruct((tensor_count, 1, 3 * width), jnp.float32),
-        in_specs=[in_smem()] + [in_vmem()] * 3,
-        out_specs=in_vmem(),
-    )(save_owner, params, moment, variance)
+        ) + lax.dynamic_index_in_dim(arrived, side, axis=0, keepdims=False).astype(jnp.float32)
+
     state = exchange(state, TENSOR)
 
     code = encode(pair_sum(1 - far))
@@ -158,16 +184,14 @@
     )(save_owner, keep(summed))
     received = exchange(pieces, TENSOR)
     squares = jnp.sum(received[:, :, width:], axis=0, keepdims=True)
-    squares = exchange(jnp.broadcast_to(squares, (4, 1, LANES)), ("dp_1", "dp_2"))
-    squares = jnp.sum(squares, axis=0, keepdims=True)
-    squares = exchange(jnp.broadcast_to(squares, (12, 1, LANES)), "dp_0")
+    squares = exchange(jnp.broadcast_to(squares, (lax.axis_size(DP), 1, LANES)), DP)
 
     return pl.pallas_call(
         functools.partial(finish, norm_limit),
         out_shape=(tile, tile, tile, jax.ShapeDtypeStruct(tile.shape, jnp.bfloat16)),
         in_specs=[in_smem()] + [in_vmem()] * 7,
         out_specs=[in_vmem()] * 4,
-    )(save_owner, *map(keep, (squares, received, state, summed)), params, moment, variance)
+    )(save_owner, *map(keep, (squares, received, state, summed, params, moment, variance)))
 
 
 def solution(mesh):

time: 103 us -> 99.8 us (0.969)
  blocking collectives: 63.7 us -> 61 us
  Pallas kernels: 3.71 us -> 5.17 us
  local copies, waits for them, and re-layouts: 1.28 us -> 0.02 us
    all_to_all x4 -> x3, blocking collectives: 63.7 us -> 61 us  [exchange(): return lax.all_to_all(array, axes, split_axis=0, concat_axis=0, tiled=True)]
    ppermute x1, waiting for transfers between devices: 5.7 us -> 7.16 us  [shards(): code = lax.ppermute(code, 'dp_1', SWAP)]
    all_to_all x1, waiting for transfers between devices: 6.85 us -> 5.41 us  [exchange(): return lax.all_to_all(array, axes, split_axis=0, concat_axis=0, tiled=True)]
    pallas_call x1, Pallas kernels: 1.42 us -> 2.84 us  [shards(): pl.pallas_call(load, out_shape=(jax.ShapeDtypeStruct((tensor_count, 1, 3...]
    squeeze x1 -> x0, local copies, waits for them, and re-layouts: 1.25 us -> none  [shards(): sent = lax.dynamic_index_in_dim(by_place, 1 - core, axis=2, keepdims=False)]
  transfers between devices with their start and end apart: 3 -> 3, of which waited for: 3 -> 3; matrix products, arithmetic and copies ran while one was open for 0% -> 0% of each run, Pallas kernels for 1% -> 0%
where the time goes in v3:
time: 99.8 us; the launch traced here: 99.4 us
  blocking collectives  61 us (61%)
  starting transfers between devices  17.9 us (18%)
  waiting for transfers between devices  14.3 us (14%)
  Pallas kernels  5.17 us (5%)
    all_to_all x3, blocking collectives, exchange(): return lax.all_to_all(array, axes, split_axis=0, concat_axis=0, tiled=True)  61 us
    ppermute x1, starting transfers between devices, shards(): arrived = lax.ppermute(sent, 'dp_2', SWAP)  12.4 us
    ppermute x1, waiting for transfers between devices, shards(): code = lax.ppermute(code, 'dp_1', SWAP)  7.16 us
    all_to_all x1, waiting for transfers between devices, exchange(): return lax.all_to_all(array, axes, split_axis=0, concat_axis=0, tiled=True)  5.41 us
    all_to_all x1, starting transfers between devices, exchange(): return lax.all_to_all(array, axes, split_axis=0, concat_axis=0, tiled=True)  3.56 us
    pallas_call x1, Pallas kernels, shards(): pl.pallas_call(load, out_shape=(jax.ShapeDtypeStruct((tensor_count, 1, 3...  2.84 us
  transfers between devices with their start and end apart: 3, of which 3 were waited for; matrix products, arithmetic and copies ran while one was open for 0% of the time, Pallas kernels for 0%

profile of v3, /device:TPU:1, one launch (start us, length us, event | category | flops | bytes accessed | tf_op | source)
XLA Modules:
  0.0 99.4 jit_solution(18311141132062630730)
XLA Ops:
  0.6 2.8 %shard_map.84 = (f32[16,1,5376]{2,1,0:T(1,128)}, bf16[2,12,8,1792]{3,2,1,0:T(8,128)(2,1)S(1)}, bf16[2,12,8,1792]{3,2,1,0:T(8,128)(2,1)S(1)}, f32[8,1792]{1,0:T(8...) custom-call(s32[1,16]{1,0:T(1,128)} %owners.5, bf16[12,2,2,8,1792]{4,3,2,1,0:T(8,128)(2,1)} %bitcast.9, ...), custom_call_target="tpu_custom_call" | custom-call | tf_op jit(solution)/shard_map/pallas_call | solution.py:151
  3.5 12.4 %collective-permute-start = (bf16[2,12,8,1792]{3,2,1,0:T(8,128)(2,1)S(1)}, bf16[2,12,8,1792]{3,2,1,0:T(8,128)(2,1)S(1)}, u32[]{:S(2)}, u32[]{:S(2)}) collective-permute-start(bf16[2,12,8,1792]{3,2,1,0:T(8,128)(2,1)S(1)} %get-tuple-element.13), channel_id=1, source_target_pairs={{0,16},{16,0},{1,17},{17,1},{2,18},{18,2},{3,19},{19,3},{4,20},{20... | collective-permute-start | bytes 2064392 | tf_op jit(solution)/shard_map/ppermute | solution.py:163
  15.9 1.7 %collective-permute-done = bf16[2,12,8,1792]{3,2,1,0:T(8,128)(2,1)S(1)} collective-permute-done((bf16[2,12,8,1792]{3,2,1,0:T(8,128)(2,1)S(1)}, bf16[2,12,8,1792]{3,2,1,0:T(8,128)(2,1)S(1)}, u32[]{:S(2)}, u32[]{:S(2)}) %collective-permute-start) | collective-permute-done | bytes 688160 | tf_op jit(solution)/shard_map/ppermute | solution.py:163
  17.6 0.1 fusion.2
  17.7 1.9 %collective-permute-start.1 = (f16[12,8,1792]{2,1,0:T(8,128)(2,1)S(1)}, f16[12,8,1792]{2,1,0:T(8,128)(2,1)S(1)}, u32[]{:S(2)}, u32[]{:S(2)}) collective-permute-start(f16[12,8,1792]{2,1,0:T(8,128)(2,1)S(1)} %fusion.2), channel_id=1, source_target_pairs={{0,32},{32,0},{1,33},{33,1},{2,34},{34,2},{3,35},{35,3},{4,36},{36... | collective-permute-start | bytes 1032200 | tf_op jit(solution)/shard_map/ppermute | solution.py:173
  19.7 3.6 %all-to-all-start = ((f32[16,1,5376]{2,1,0:T(1,128)}), f32[16,1,5376]{2,1,0:T(1,128)S(1)}, u32[]{:S(2)}, u32[]{:S(2)}) async-start(f32[16,1,5376]{2,1,0:T(1,128)} %get-tuple-element.14), calls=%async_computation | async-start | bytes 688128 | tf_op jit(solution)/shard_map/all_to_all | solution.py:48
  23.2 7.2 %collective-permute-done.1 = f16[12,8,1792]{2,1,0:T(8,128)(2,1)S(1)} collective-permute-done((f16[12,8,1792]{2,1,0:T(8,128)(2,1)S(1)}, f16[12,8,1792]{2,1,0:T(8,128)(2,1)S(1)}, u32[]{:S(2)}, u32[]{:S(2)}) %collective-permute-start.1) | collective-permute-done | bytes 344096 | tf_op jit(solution)/shard_map/ppermute | solution.py:173
  30.4 0.2 fusion.1
  30.6 5.4 %all-to-all-done.state = f32[16,1,5376]{2,1,0:T(1,128)S(1)} async-done(((f32[16,1,5376]{2,1,0:T(1,128)}), f32[16,1,5376]{2,1,0:T(1,128)S(1)}, u32[]{:S(2)}, u32[]{:S(2)}) %all-to-all-start) | async-done | bytes 344096 | tf_op jit(solution)/shard_map/all_to_all | solution.py:48
  36.0 25.9 %all_to_all.20 = f16[12,8,1792]{2,1,0:T(8,128)(2,1)S(1)} all-to-all(f16[12,8,1792]{2,1,0:T(8,128)(2,1)S(1)} %fusion.1), channel_id=1, replica_groups=mesh['dp_0'=12,'dp_1'=2,'dp_2'=2,'tensor_0'=8,'tensor_1'=2] {'dp_0'}, dimensions={0} | all-to-all | bytes 688128 | tf_op jit(solution)/shard_map/all_to_all | solution.py:48
  61.9 0.1 multiply_reduce_fusion.summed
  62.0 0.7 shard_map.85
  62.7 15.1 %all_to_all.21.received = f32[16,1,1920]{2,1,0:T(1,128)S(1)} all-to-all(f32[16,1,1920]{2,1,0:T(1,128)S(1)} %shard_map.85), channel_id=1, replica_groups=mesh['dp_0'=12,'dp_1'=2,'dp_2'=2,'tensor_0'=8,'tensor_1'=2] {'tensor_0',..., dimensions={0} | all-to-all | bytes 245760 | tf_op jit(solution)/shard_map/all_to_all | solution.py:48
  77.9 19.9 %all_to_all.22.squares = f32[48,1,128]{2,1,0:T(1,128)S(1)} all-to-all(f32[48,1,128]{2,1,0:T(1,128)S(1)} %broadcast_in_dim.2), channel_id=1, replica_groups=mesh['dp_0'=12,'dp_1'=2,'dp_2'=2,'tensor_0'=8,'tensor_1'=2] {'dp_0','dp_..., dimensions={0} | all-to-all | bytes 49152 | tf_op jit(solution)/shard_map/all_to_all | solution.py:48
  97.8 1.6 %shard_map.86 = (f32[8,1792]{1,0:T(8,128)}, f32[8,1792]{1,0:T(8,128)}, f32[8,1792]{1,0:T(8,128)}, bf16[8,1792]{1,0:T(8,128)(2,1)}) custom-call(s32[1,16]{1,0:T(1,128)} %owners.5, f32[48,1,128]{2,1,0:T(1,128)S(1)} %all_to_all.22.squares, f32[16,1,1920]{2,1,0:T(1,128)S(1)} %all_to_all.21.received, f32[16,1,5376]{2,1,0:T(1,128)S(1)} %all-to-all-done.state, ...), custom_call_target="tpu_custom_call" | custom-call | tf_op jit(solution)/shard_map/pallas_call | solution.py:189
  (2 shorter events, 0.0 us)
Async XLA Ops:
  3.5 14.1 %collective-permute-start = (bf16[2,12,8,1792]{3,2,1,0:T(8,128)(2,1)S(1)}, bf16[2,12,8,1792]{3,2,1,0:T(8,128)(2,1)S(1)}, u32[]{:S(2)}, u32[]{:S(2)}) collective-permute-start(bf16[2,12,8,1792]{3,2,1,0:T(8,128)(2,1)S(1)} %get-tuple-element.13), channel_id=1, source_target_pairs={{0,16},{16,0},{1,17},{17,1},{2,18},{18,2},{3,19},{19,3},{4,20},{20... | collective-permute-start | bytes 2064392 | tf_op jit(solution)/shard_map/ppermute | solution.py:163
  17.7 12.7 %collective-permute-start.1 = (f16[12,8,1792]{2,1,0:T(8,128)(2,1)S(1)}, f16[12,8,1792]{2,1,0:T(8,128)(2,1)S(1)}, u32[]{:S(2)}, u32[]{:S(2)}) collective-permute-start(f16[12,8,1792]{2,1,0:T(8,128)(2,1)S(1)} %fusion.2), channel_id=1, source_target_pairs={{0,32},{32,0},{1,33},{33,1},{2,34},{34,2},{3,35},{35,3},{4,36},{36... | collective-permute-start | bytes 1032200 | tf_op jit(solution)/shard_map/ppermute | solution.py:173
  19.7 16.3 %all-to-all-start = ((f32[16,1,5376]{2,1,0:T(1,128)}), f32[16,1,5376]{2,1,0:T(1,128)S(1)}, u32[]{:S(2)}, u32[]{:S(2)}) async-start(f32[16,1,5376]{2,1,0:T(1,128)} %get-tuple-element.14), calls=%async_computation | async-start | bytes 688128 | tf_op jit(solution)/shard_map/all_to_all | solution.py:48

commit v4 on v3

--- a/solution.py
+++ b/solution.py
@@ -60,10 +60,7 @@
     return pl.BlockSpec(memory_space=pltpu.SMEM)
 
 
-def load(owners, grads, params, moment, variance, state, kept, sent, *rest):
-    own_rows, width = params.shape
-    halves = owners.shape[1] // own_rows
-    half = lax.axis_index(TENSOR) // own_rows
+def load(grads, params, moment, variance, kept, sent, *rest):
     core = lax.axis_index("dp_2")
     own, semaphores = rest[:3], rest[3]
     copies = [
@@ -81,16 +78,22 @@
             )
     for copy in copies:
         copy.start()
-    for place, array in enumerate(own):
-        copies[place].wait()
-        for row in range(own_rows):
-            slot = owners[0, row * halves + half]
-            state[slot, :, place * width : (place + 1) * width] = array[row : row + 1, :]
-    for copy in copies[3:]:
+    for copy in copies:
         copy.wait()
 
 
-def pack_summed(owners, summed, out):
+def pack_state(owners, params, moment, variance, out):
+    own_rows, width = params.shape
+    halves = owners.shape[1] // own_rows
+    half = lax.axis_index(TENSOR) // own_rows
+    for row in range(own_rows):
+        slot = owners[0, row * halves + half]
+        for place, array in enumerate((params, moment, variance)):
+            start = (place + 1) * width
+            out[slot, :, start : start + width] = array[row : row + 1, :]
+
+
+def pack_summed(owners, summed, state, out):
     own_rows, width = summed.shape
     halves = owners.shape[1] // own_rows
     half = lax.axis_index(TENSOR) // own_rows
@@ -100,13 +103,13 @@
         squares = squares + tile * tile
     squares = jnp.sum(squares, axis=0, keepdims=True)
     for slot in range(out.shape[0]):
-        out[slot, :, width:] = squares
+        out[slot, :, 4 * width :] = squares
     for row in range(own_rows):
         slot = owners[0, row * halves + half]
         out[slot, :, :width] = summed[row : row + 1, :]
 
 
-def finish(norm_limit, owners, squares, received, state, summed, params, moment, variance,
+def finish(norm_limit, owners, squares, received, summed, params, moment, variance,
            fresh_out, moment_out, variance_out, groups_out):
     own_rows, width = params.shape
     tensor_count = owners.shape[1]
@@ -124,14 +127,13 @@
     moment_out[...] = moment_next
     variance_out[...] = variance_next
 
-    def rows(array, start):
+    def rows(place):
+        start = place * width
         return jnp.concatenate(
-            [array[first + row, :, start : start + width] for row in range(own_rows)], axis=0
+            [received[first + row, :, start : start + width] for row in range(own_rows)], axis=0
         )
 
-    groups = adam_update(
-        rows(received, 0), rows(state, 0), rows(state, width), rows(state, 2 * width), clip_scale
-    )[0]
+    groups = adam_update(*map(rows, range(4)), clip_scale)[0]
     groups_out[...] = groups.astype(groups_out.dtype)
 
 
@@ -148,18 +150,17 @@
     core_count = lax.axis_size("dp_2")
     far_count = lax.axis_size("dp_1")
     part = pltpu.VMEM((far_count, by_place.shape[0], own_rows, width), grads.dtype)
-    state, kept, sent, params, moment, variance = pl.pallas_call(
+    kept, sent, params, moment, variance = pl.pallas_call(
         load,
         out_shape=(
-            jax.ShapeDtypeStruct((tensor_count, 1, 3 * width), jnp.float32),
             part,
             part,
             *[pltpu.VMEM(tile.shape, tile.dtype)] * 3,
         ),
-        in_specs=[in_smem()] + [pl.BlockSpec(memory_space=pl.ANY)] * 4,
-        out_specs=[in_vmem()] * 6,
+        in_specs=[pl.BlockSpec(memory_space=pl.ANY)] * 4,
+        out_specs=[in_vmem()] * 5,
         scratch_shapes=[pltpu.SemaphoreType.DMA((3 + far_count * core_count,))],
-    )(save_owner, by_place, params, moment, variance)
+    )(by_place, params, moment, variance)
     arrived = lax.ppermute(sent, "dp_2", SWAP)
 
     def pair_sum(side):
@@ -167,31 +168,37 @@
             jnp.float32
         ) + lax.dynamic_index_in_dim(arrived, side, axis=0, keepdims=False).astype(jnp.float32)
 
-    state = exchange(state, TENSOR)
+    piece = pltpu.VMEM((tensor_count, 1, 4 * width + LANES), jnp.float32)
+    state = pl.pallas_call(
+        pack_state,
+        out_shape=piece,
+        in_specs=[in_smem()] + [in_vmem()] * 3,
+        out_specs=in_vmem(),
+    )(save_owner, *map(keep, (params, moment, variance)))
 
     code = encode(pair_sum(1 - far))
     code = lax.ppermute(code, "dp_1", SWAP)
     four = pair_sum(far) + decode(code)
 
-    codes, state = lax.optimization_barrier((encode(four), state))
-    summed = jnp.sum(decode(exchange(codes, "dp_0")), axis=0)
+    summed = jnp.sum(decode(exchange(encode(four), "dp_0")), axis=0)
 
     pieces = pl.pallas_call(
         pack_summed,
-        out_shape=pltpu.VMEM((tensor_count, 1, width + LANES), jnp.float32),
-        in_specs=[in_smem(), in_vmem()],
+        out_shape=piece,
+        in_specs=[in_smem(), in_vmem(), in_vmem()],
         out_specs=in_vmem(),
-    )(save_owner, keep(summed))
+        input_output_aliases={2: 0},
+    )(save_owner, keep(summed), keep(state))
     received = exchange(pieces, TENSOR)
-    squares = jnp.sum(received[:, :, width:], axis=0, keepdims=True)
+    squares = jnp.sum(received[:, :, 4 * width :], axis=0, keepdims=True)
     squares = exchange(jnp.broadcast_to(squares, (lax.axis_size(DP), 1, LANES)), DP)
 
     return pl.pallas_call(
         functools.partial(finish, norm_limit),
         out_shape=(tile, tile, tile, jax.ShapeDtypeStruct(tile.shape, jnp.bfloat16)),
-        in_specs=[in_smem()] + [in_vmem()] * 7,
+        in_specs=[in_smem()] + [in_vmem()] * 6,
         out_specs=[in_vmem()] * 4,
-    )(save_owner, *map(keep, (squares, received, state, summed, params, moment, variance)))
+    )(save_owner, *map(keep, (squares, received, summed, params, moment, variance)))
 
 
 def solution(mesh):

time: 99.8 us -> 99.5 us (level)
  blocking collectives: 61 us -> 45 us
  waiting for transfers between devices: 14.3 us -> 27.6 us
  starting transfers between devices: 17.9 us -> 20.2 us
    all_to_all x3 -> x2, blocking collectives: 61 us -> 45 us  [exchange(): return lax.all_to_all(array, axes, split_axis=0, concat_axis=0, tiled=True)]
    all_to_all x1, waiting for transfers between devices: 5.41 us -> 15.2 us  [exchange(): return lax.all_to_all(array, axes, split_axis=0, concat_axis=0, tiled=True)]
    ppermute x1, waiting for transfers between devices: 7.16 us -> 10.7 us  [shards(): code = lax.ppermute(code, 'dp_1', SWAP)]
    all_to_all x1, starting transfers between devices: 3.56 us -> 5.89 us  [exchange(): return lax.all_to_all(array, axes, split_axis=0, concat_axis=0, tiled=True)]
    pallas_call x2 -> x3, Pallas kernels: 3.53 us -> 2.86 us  [the longest x1 1.46 us: shards(): pl.pallas_call(load, out_shape=(part, part, *[pltpu.VMEM(tile.shape, tile...]
  transfers between devices with their start and end apart: 3 -> 3, of which waited for: 3 -> 3; matrix products, arithmetic and copies ran while one was open for 0% -> 0% of each run, Pallas kernels for 0% -> 1%
where the time goes in v4:
time: 99.5 us; the launch traced here: 99.2 us
  blocking collectives  45 us (45%)
  waiting for transfers between devices  27.6 us (28%)
  starting transfers between devices  20.2 us (20%)
  Pallas kernels  4.5 us (5%)
  other arithmetic  1.15 us (1%)
    all_to_all x2, blocking collectives, exchange(): return lax.all_to_all(array, axes, split_axis=0, concat_axis=0, tiled=True)  45 us
    all_to_all x1, waiting for transfers between devices, exchange(): return lax.all_to_all(array, axes, split_axis=0, concat_axis=0, tiled=True)  15.2 us
    ppermute x1, starting transfers between devices, shards(): arrived = lax.ppermute(sent, 'dp_2', SWAP)  12.4 us
    ppermute x1, waiting for transfers between devices, shards(): code = lax.ppermute(code, 'dp_1', SWAP)  10.7 us
    all_to_all x1, starting transfers between devices, exchange(): return lax.all_to_all(array, axes, split_axis=0, concat_axis=0, tiled=True)  5.89 us
  transfers between devices with their start and end apart: 3, of which 3 were waited for; matrix products, arithmetic and copies ran while one was open for 0% of the time, Pallas kernels for 1%

profile of v4, /device:TPU:1, one launch (start us, length us, event | category | flops | bytes accessed | tf_op | source)
XLA Modules:
  0.0 99.2 jit_solution(16236448073844504223)
XLA Ops:
  0.6 1.5 %shard_map.84 = (bf16[2,12,8,1792]{3,2,1,0:T(8,128)(2,1)S(1)}, bf16[2,12,8,1792]{3,2,1,0:T(8,128)(2,1)S(1)}, f32[8,1792]{1,0:T(8,128)S(1)}, f32[8,1792]{1,0:T(8,128)S(1)}, f32[8,1792]{1,0:T(8,128)S(1)}) custom-call(bf16[12,2,2,8,1792]{4,3,2,1,0:T(8,128)(2,1)} %bitcast.9, f32[8,1792]{1,0:T(8,128)} %params.1, f32[8,1792]{1,0:T(8,128)} %moment.1, ...), custom_call_target="tpu_custom_call" | custom-call | tf_op jit(solution)/shard_map/pallas_call | solution.py:153
  2.1 12.4 %collective-permute-start = (bf16[2,12,8,1792]{3,2,1,0:T(8,128)(2,1)S(1)}, bf16[2,12,8,1792]{3,2,1,0:T(8,128)(2,1)S(1)}, u32[]{:S(2)}, u32[]{:S(2)}) collective-permute-start(bf16[2,12,8,1792]{3,2,1,0:T(8,128)(2,1)S(1)} %get-tuple-element.10), channel_id=1, source_target_pairs={{0,16},{16,0},{1,17},{17,1},{2,18},{18,2},{3,19},{19,3},{4,20},{20... | collective-permute-start | bytes 2064392 | tf_op jit(solution)/shard_map/ppermute | solution.py:164
  14.5 1.7 %collective-permute-done = bf16[2,12,8,1792]{3,2,1,0:T(8,128)(2,1)S(1)} collective-permute-done((bf16[2,12,8,1792]{3,2,1,0:T(8,128)(2,1)S(1)}, bf16[2,12,8,1792]{3,2,1,0:T(8,128)(2,1)S(1)}, u32[]{:S(2)}, u32[]{:S(2)}) %collective-permute-start) | collective-permute-done | bytes 688160 | tf_op jit(solution)/shard_map/ppermute | solution.py:164
  16.2 0.1 fusion.2
  16.4 1.9 %collective-permute-start.1 = (f16[12,8,1792]{2,1,0:T(8,128)(2,1)S(1)}, f16[12,8,1792]{2,1,0:T(8,128)(2,1)S(1)}, u32[]{:S(2)}, u32[]{:S(2)}) collective-permute-start(f16[12,8,1792]{2,1,0:T(8,128)(2,1)S(1)} %fusion.2), channel_id=1, source_target_pairs={{0,32},{32,0},{1,33},{33,1},{2,34},{34,2},{3,35},{35,3},{4,36},{36... | collective-permute-start | bytes 1032200 | tf_op jit(solution)/shard_map/ppermute | solution.py:180
  18.3 10.7 %collective-permute-done.1 = f16[12,8,1792]{2,1,0:T(8,128)(2,1)S(1)} collective-permute-done((f16[12,8,1792]{2,1,0:T(8,128)(2,1)S(1)}, f16[12,8,1792]{2,1,0:T(8,128)(2,1)S(1)}, u32[]{:S(2)}, u32[]{:S(2)}) %collective-permute-start.1) | collective-permute-done | bytes 344096 | tf_op jit(solution)/shard_map/ppermute | solution.py:180
  29.0 0.9 fusion.1
  29.9 5.9 %all-to-all-start = ((f16[12,8,1792]{2,1,0:T(8,128)(2,1)}), f16[12,8,1792]{2,1,0:T(8,128)(2,1)S(1)}, u32[]{:S(2)}, u32[]{:S(2)}) async-start(f16[12,8,1792]{2,1,0:T(8,128)(2,1)} %fusion.1), calls=%async_computation | async-start | bytes 688128 | tf_op jit(solution)/shard_map/all_to_all | solution.py:48
  35.8 0.7 shard_map.85.state
  36.5 15.2 %all-to-all-done = f16[12,8,1792]{2,1,0:T(8,128)(2,1)S(1)} async-done(((f16[12,8,1792]{2,1,0:T(8,128)(2,1)}), f16[12,8,1792]{2,1,0:T(8,128)(2,1)S(1)}, u32[]{:S(2)}, u32[]{:S(2)}) %all-to-all-start) | async-done | bytes 344096 | tf_op jit(solution)/shard_map/all_to_all | solution.py:48
  51.7 0.1 multiply_reduce_fusion.summed
  51.8 0.7 shard_map.86
  52.5 19.1 %all_to_all.15.received = f32[16,1,7296]{2,1,0:T(1,128)S(1)} all-to-all(f32[16,1,7296]{2,1,0:T(1,128)S(1)} %shard_map.86), channel_id=1, replica_groups=mesh['dp_0'=12,'dp_1'=2,'dp_2'=2,'tensor_0'=8,'tensor_1'=2] {'tensor_0',..., dimensions={0} | all-to-all | bytes 933888 | tf_op jit(solution)/shard_map/all_to_all | solution.py:48
  71.7 25.8 %all_to_all.16.squares = f32[48,1,128]{2,1,0:T(1,128)S(1)} all-to-all(f32[48,1,128]{2,1,0:T(1,128)S(1)} %broadcast_in_dim.2), channel_id=1, replica_groups=mesh['dp_0'=12,'dp_1'=2,'dp_2'=2,'tensor_0'=8,'tensor_1'=2] {'dp_0','dp_..., dimensions={0} | all-to-all | bytes 49152 | tf_op jit(solution)/shard_map/all_to_all | solution.py:48
  97.5 1.6 %shard_map.87 = (f32[8,1792]{1,0:T(8,128)}, f32[8,1792]{1,0:T(8,128)}, f32[8,1792]{1,0:T(8,128)}, bf16[8,1792]{1,0:T(8,128)(2,1)}) custom-call(s32[1,16]{1,0:T(1,128)} %owners.5, f32[48,1,128]{2,1,0:T(1,128)S(1)} %all_to_all.16.squares, f32[16,1,7296]{2,1,0:T(1,128)S(1)} %all_to_all.15.received, f32[8,1792]{1,0:T(8,128)S(1)} %multiply_reduce_fusion.summed, ...), custom_call_target="tpu_custom_call" | custom-call | tf_op jit(solution)/shard_map/pallas_call | solution.py:196
  (2 shorter events, 0.0 us)
Async XLA Ops:
  2.1 14.1 %collective-permute-start = (bf16[2,12,8,1792]{3,2,1,0:T(8,128)(2,1)S(1)}, bf16[2,12,8,1792]{3,2,1,0:T(8,128)(2,1)S(1)}, u32[]{:S(2)}, u32[]{:S(2)}) collective-permute-start(bf16[2,12,8,1792]{3,2,1,0:T(8,128)(2,1)S(1)} %get-tuple-element.10), channel_id=1, source_target_pairs={{0,16},{16,0},{1,17},{17,1},{2,18},{18,2},{3,19},{19,3},{4,20},{20... | collective-permute-start | bytes 2064392 | tf_op jit(solution)/shard_map/ppermute | solution.py:164
  16.4 12.6 %collective-permute-start.1 = (f16[12,8,1792]{2,1,0:T(8,128)(2,1)S(1)}, f16[12,8,1792]{2,1,0:T(8,128)(2,1)S(1)}, u32[]{:S(2)}, u32[]{:S(2)}) collective-permute-start(f16[12,8,1792]{2,1,0:T(8,128)(2,1)S(1)} %fusion.2), channel_id=1, source_target_pairs={{0,32},{32,0},{1,33},{33,1},{2,34},{34,2},{3,35},{35,3},{4,36},{36... | collective-permute-start | bytes 1032200 | tf_op jit(solution)/shard_map/ppermute | solution.py:180
  29.9 21.8 %all-to-all-start = ((f16[12,8,1792]{2,1,0:T(8,128)(2,1)}), f16[12,8,1792]{2,1,0:T(8,128)(2,1)S(1)}, u32[]{:S(2)}, u32[]{:S(2)}) async-start(f16[12,8,1792]{2,1,0:T(8,128)(2,1)} %fusion.1), calls=%async_computation | async-start | bytes 688128 | tf_op jit(solution)/shard_map/all_to_all | solution.py:48

commit v5 on v4

v5 whole, which is shorter than its diff:
```python
import functools
import math

import jax
import jax.numpy as jnp
from jax import lax
from jax.experimental import pallas as pl
from jax.experimental.pallas import tpu as pltpu
from jax.sharding import Mesh
from jax.sharding import PartitionSpec as P


TENSOR = ("tensor_0", "tensor_1")
DP = ("dp_0", "dp_1", "dp_2")
DP_TENSOR = ("dp_0", "dp_1", "dp_2", "tensor_0", "tensor_1")
SWAP = ((0, 1), (1, 0))
LANES = 128

learn_rate = 0.05
beta_first = 0.9
beta_second = 0.999
adam_step = 1000.0
adam_eps = 1e-08
norm_eps = 1e-06

SPREAD = 16.0


def encode(value):
    return (value * SPREAD).astype(jnp.float16)


def decode(code):
    return code.astype(jnp.float32) * (1.0 / SPREAD)


def adam_update(summed, params, moment, variance, clip_scale):
    scaled = clip_scale * summed
    moment_next = beta_first * moment + (1.0 - beta_first) * scaled
    variance_next = beta_second * variance + (1.0 - beta_second) * scaled * scaled
    first_fix = 1.0 - beta_first**adam_step
    second_fix = 1.0 - beta_second**adam_step
    update = moment_next / first_fix / (jnp.sqrt(variance_next / second_fix) + adam_eps)
    return (params - learn_rate * update, moment_next, variance_next)


def exchange(array, axes):
    return lax.all_to_all(array, axes, split_axis=0, concat_axis=0, tiled=True)


def in_vmem():
    return pl.BlockSpec(memory_space=pltpu.VMEM)


def keep(array):
    return pltpu.with_memory_space_constraint(array, pltpu.VMEM)


def in_smem():
    return pl.BlockSpec(memory_space=pltpu.SMEM)


def load_first(grads, out, semaphore):
    far, core = lax.axis_index("dp_1"), lax.axis_index("dp_2")
    copy = pltpu.make_async_copy(grads.at[:, 1 - far, 1 - core], out, semaphore)
    copy.start()
    copy.wait()


def load_rest(grads, params, moment, variance, sent, kept_first, kept_rest, *rest):
    far, core = lax.axis_index("dp_1"), lax.axis_index("dp_2")
    semaphores = rest[3]
    pairs = (
        (grads.at[:, 1 - far, core], kept_first),
        (grads.at[:, far, 1 - core], sent),
        (grads.at[:, far, core], kept_rest),
        *zip((params, moment, variance), rest[:3]),
    )
    copies = [
        pltpu.make_async_copy(source, place, semaphores.at[index])
        for index, (source, place) in enumerate(pairs)
    ]
    for copy in copies:
        copy.start()
    for copy in copies:
        copy.wait()


def pack_state(owners, params, moment, variance, out):
    own_rows, width = params.shape
    halves = owners.shape[1] // own_rows
    half = lax.axis_index(TENSOR) // own_rows
    for row in range(own_rows):
        slot = owners[0, row * halves + half]
        for place, array in enumerate((params, moment, variance)):
            start = (place + 1) * width
            out[slot, :, start : start + width] = array[row : row + 1, :]


def pack_summed(owners, summed, state, out, held_owners, semaphore):
    own_rows, width = summed.shape
    copy = pltpu.make_async_copy(owners, held_owners, semaphore)
    copy.start()
    halves = owners.shape[1] // own_rows
    half = lax.axis_index(TENSOR) // own_rows
    squares = jnp.zeros((own_rows, LANES), jnp.float32)
    for start in range(0, width, LANES):
        tile = summed[:, start : start + LANES]
        squares = squares + tile * tile
    squares = jnp.sum(squares, axis=0, keepdims=True)
    for slot in range(out.shape[0]):
        out[slot, :, 4 * width :] = squares
    copy.wait()
    for row in range(own_rows):
        slot = held_owners[0, row * halves + half]
        out[slot, :, :width] = summed[row : row + 1, :]


def finish(norm_limit, owners, squares, received, summed, params, moment, variance, *rest):
    outs, held, held_owners, semaphores = rest[:4], rest[4:8], rest[8], rest[9]
    own_rows, width = params.shape
    tensor_count = owners.shape[1]
    halves = tensor_count // own_rows
    owners_copy = pltpu.make_async_copy(owners, held_owners, semaphores.at[4])
    owners_copy.start()
    copies = [
        pltpu.make_async_copy(source, out, semaphores.at[index])
        for index, (source, out) in enumerate(zip(held, outs))
    ]
    norm = jnp.sqrt(jnp.sum(jnp.sum(squares[...], axis=0), axis=1, keepdims=True))
    clip_scale = jnp.minimum(1.0, norm_limit / (norm + norm_eps))
    results = adam_update(summed[...], params[...], moment[...], variance[...], clip_scale)
    for copy, place, result in zip(copies, held, results):
        place[...] = result
        copy.start()

    owners_copy.wait()
    place = lax.axis_index(TENSOR)
    first = jnp.int32(0)
    for group in range(tensor_count):
        first = jnp.where(held_owners[0, group] == place, group % halves * own_rows, first)

    def rows(place):
        start = place * width
        return jnp.concatenate(
            [received[first + row, :, start : start + width] for row in range(own_rows)], axis=0
        )

    groups = adam_update(*map(rows, range(4)), clip_scale)[0]
    held[3][...] = groups.astype(held[3].dtype)
    copies[3].start()
    for copy in copies:
        copy.wait()


def shards(grads, params, moment, variance, save_owner):
    own_rows, width = params.shape
    tensor_count = lax.axis_size(TENSOR)
    norm_limit = math.sqrt(float(grads.shape[1] * width * tensor_count))
    tile = jax.ShapeDtypeStruct((own_rows, width), jnp.float32)

    by_place = grads[0].reshape(
        lax.axis_size("dp_0"), lax.axis_size("dp_1"), lax.axis_size("dp_2"), own_rows, width
    )
    part = pltpu.VMEM((by_place.shape[0], own_rows, width), grads.dtype)
    in_hbm = pl.BlockSpec(memory_space=pl.ANY)

    sent = pl.pallas_call(
        load_first,
        out_shape=part,
        in_specs=[in_hbm],
        out_specs=in_vmem(),
        scratch_shapes=[pltpu.SemaphoreType.DMA(())],
    )(by_place)
    arrived_first = lax.ppermute(sent, "dp_2", SWAP)
    sent, kept_first, kept_rest, params, moment, variance = pl.pallas_call(
        load_rest,
        out_shape=(*[part] * 3, *[pltpu.VMEM(tile.shape, tile.dtype)] * 3),
        in_specs=[in_hbm] * 4,
        out_specs=[in_vmem()] * 6,
        scratch_shapes=[pltpu.SemaphoreType.DMA((6,))],
    )(by_place, params, moment, variance)
    arrived_rest = lax.ppermute(sent, "dp_2", SWAP)

    def pair_sum(kept, arrived):
        return kept.astype(jnp.float32) + arrived.astype(jnp.float32)

    piece = pltpu.VMEM((tensor_count, 1, 4 * width + LANES), jnp.float32)
    state = pl.pallas_call(
        pack_state,
        out_shape=piece,
        in_specs=[in_smem()] + [in_vmem()] * 3,
        out_specs=in_vmem(),
    )(save_owner, *map(keep, (params, moment, variance)))

    code = encode(pair_sum(kept_first, arrived_first))
    code = lax.ppermute(code, "dp_1", SWAP)
    four = pair_sum(kept_rest, arrived_rest) + decode(code)

    summed = jnp.sum(decode(exchange(encode(four), "dp_0")), axis=0)

    pieces = pl.pallas_call(
        pack_summed,
        out_shape=piece,
        in_specs=[in_hbm, in_vmem(), in_vmem()],
        out_specs=in_vmem(),
        scratch_shapes=[pltpu.SMEM(save_owner.shape, jnp.int32), pltpu.SemaphoreType.DMA(())],
        input_output_aliases={2: 0},
    )(save_owner, keep(summed), keep(state))
    received = exchange(pieces, TENSOR)
    squares = jnp.sum(received[:, :, 4 * width :], axis=0, keepdims=True)
    squares = exchange(jnp.broadcast_to(squares, (lax.axis_size(DP), 1, LANES)), DP)

    outs = [tile, tile, tile, jax.ShapeDtypeStruct(tile.shape, jnp.bfloat16)]
    return pl.pallas_call(
        functools.partial(finish, norm_limit),
        out_shape=outs,
        in_specs=[in_hbm] + [in_vmem()] * 6,
        out_specs=[in_hbm] * 4,
        scratch_shapes=[
            *[pltpu.VMEM(out.shape, out.dtype) for out in outs],
            pltpu.SMEM(save_owner.shape, jnp.int32),
            pltpu.SemaphoreType.DMA((5,)),
        ],
    )(save_owner, *map(keep, (squares, received, summed, params, moment, variance)))


def solution(mesh):
    torus = Mesh(
        mesh.devices.reshape(12, 2, 2, 8, 2), ("dp_0", "dp_1", "dp_2", "tensor_0", "tensor_1")
    )
    return jax.shard_map(
        shards,
        mesh=torus,
        in_specs=(P(DP, None, TENSOR), P(DP, TENSOR), P(DP, TENSOR), P(DP, TENSOR), P(DP, None)),
        out_specs=(P(DP, TENSOR), P(DP, TENSOR), P(DP, TENSOR), P(DP_TENSOR, None)),
        check_vma=False,
    )
```

time: 99.5 us -> 100 us (level)
  starting transfers between devices: 20.2 us -> 22.1 us
  waiting for transfers between devices: 27.6 us -> 25.8 us
    ppermute x1 -> x2, starting transfers between devices: 12.4 us -> 14.3 us  [the longest x1 12.4 us: shards(): arrived_first = lax.ppermute(sent, 'dp_2', SWAP)]
    ppermute x1 -> x2, waiting for transfers between devices: 1.74 us -> 0.01 us  [the longest x1 0.01 us: shards(): arrived_rest = lax.ppermute(sent, 'dp_2', SWAP)]
    pallas_call x3 -> x4, Pallas kernels: 3.79 us -> 4.41 us  [the longest x1 1.46 us: shards(): pl.pallas_call(functools.partial(finish, norm_limit), out_shape=outs, in_...]
  transfers between devices with their start and end apart: 3 -> 4, of which waited for: 3 -> 2; matrix products, arithmetic and copies ran while one was open for 0% -> 0% of each run, Pallas kernels for 1% -> 2%
where the time goes in v5:
time: 100 us; the launch traced here: 99.8 us
  blocking collectives  45 us (45%)
  waiting for transfers between devices  25.8 us (26%)
  starting transfers between devices  22.1 us (22%)
  Pallas kernels  5.12 us (5%)
  other arithmetic  1.15 us (1%)
    all_to_all x2, blocking collectives, exchange(): return lax.all_to_all(array, axes, split_axis=0, concat_axis=0, tiled=True)  45 us
    all_to_all x1, waiting for transfers between devices, exchange(): return lax.all_to_all(array, axes, split_axis=0, concat_axis=0, tiled=True)  15.2 us
    ppermute x1, starting transfers between devices, shards(): arrived_first = lax.ppermute(sent, 'dp_2', SWAP)  12.4 us
    ppermute x1, waiting for transfers between devices, shards(): code = lax.ppermute(code, 'dp_1', SWAP)  10.6 us
    all_to_all x1, starting transfers between devices, exchange(): return lax.all_to_all(array, axes, split_axis=0, concat_axis=0, tiled=True)  5.89 us
  transfers between devices with their start and end apart: 4, of which 2 were waited for; matrix products, arithmetic and copies ran while one was open for 0% of the time, Pallas kernels for 2%

profile of v5, /device:TPU:1, one launch (start us, length us, event | category | flops | bytes accessed | tf_op | source)
XLA Modules:
  0.0 99.8 jit_solution(8665512745597497489)
XLA Ops:
  0.6 1.0 %shard_map.85 = bf16[12,8,1792]{2,1,0:T(8,128)(2,1)S(1)} custom-call(bf16[12,2,2,8,1792]{4,3,2,1,0:T(8,128)(2,1)} %bitcast.1), custom_call_target="tpu_custom_call" | custom-call | tf_op jit(solution)/shard_map/pallas_call | solution.py:168
  1.6 12.4 %collective-permute-start.1 = (bf16[12,8,1792]{2,1,0:T(8,128)(2,1)S(1)}, bf16[12,8,1792]{2,1,0:T(8,128)(2,1)S(1)}, u32[]{:S(2)}, u32[]{:S(2)}) collective-permute-start(bf16[12,8,1792]{2,1,0:T(8,128)(2,1)S(1)} %shard_map.85), channel_id=1, source_target_pairs={{0,16},{16,0},{1,17},{17,1},{2,18},{18,2},{3,19},{19,3},{4,20},{20... | collective-permute-start | bytes 1032200 | tf_op jit(solution)/shard_map/ppermute | solution.py:175
  14.0 1.3 %shard_map.84 = (bf16[12,8,1792]{2,1,0:T(8,128)(2,1)S(1)}, bf16[12,8,1792]{2,1,0:T(8,128)(2,1)S(1)}, bf16[12,8,1792]{2,1,0:T(8,128)(2,1)S(1)}, f32[8,1792]{1,0:T...) custom-call(bf16[12,2,2,8,1792]{4,3,2,1,0:T(8,128)(2,1)} %bitcast.2, f32[8,1792]{1,0:T(8,128)} %params.1, ...), custom_call_target="tpu_custom_call" | custom-call | tf_op jit(solution)/shard_map/pallas_call | solution.py:176
  15.3 1.9 %collective-permute-start = (bf16[12,8,1792]{2,1,0:T(8,128)(2,1)S(1)}, bf16[12,8,1792]{2,1,0:T(8,128)(2,1)S(1)}, u32[]{:S(2)}, u32[]{:S(2)}) collective-permute-start(bf16[12,8,1792]{2,1,0:T(8,128)(2,1)S(1)} %get-tuple-element.11), channel_id=1, source_target_pairs={{0,16},{16,0},{1,17},{17,1},{2,18},{18,2},{3,19},{19,3},{4,20},{20... | collective-permute-start | bytes 1032200 | tf_op jit(solution)/shard_map/ppermute | solution.py:183
  17.2 0.0 collective-permute-done.1
  17.2 0.1 multiply_convert_fusion.1
  17.4 1.9 %collective-permute-start.2 = (f16[12,8,1792]{2,1,0:T(8,128)(2,1)S(1)}, f16[12,8,1792]{2,1,0:T(8,128)(2,1)S(1)}, u32[]{:S(2)}, u32[]{:S(2)}) collective-permute-start(f16[12,8,1792]{2,1,0:T(8,128)(2,1)S(1)} %multiply_convert_fusion.1), channel_id=1, source_target_pairs={{0,32},{32,0},{1,33},{33,1},{2,34},{34,2},{3,35},{35,3},{4,36},{36... | collective-permute-start | bytes 1032200 | tf_op jit(solution)/shard_map/ppermute | solution.py:197
  19.3 0.0 collective-permute-done
  19.3 10.6 %collective-permute-done.2 = f16[12,8,1792]{2,1,0:T(8,128)(2,1)S(1)} collective-permute-done((f16[12,8,1792]{2,1,0:T(8,128)(2,1)S(1)}, f16[12,8,1792]{2,1,0:T(8,128)(2,1)S(1)}, u32[]{:S(2)}, u32[]{:S(2)}) %collective-permute-start.2) | collective-permute-done | bytes 344096 | tf_op jit(solution)/shard_map/ppermute | solution.py:197
  29.9 0.9 multiply_convert_fusion
  30.8 5.9 %all-to-all-start = ((f16[12,8,1792]{2,1,0:T(8,128)(2,1)}), f16[12,8,1792]{2,1,0:T(8,128)(2,1)S(1)}, u32[]{:S(2)}, u32[]{:S(2)}) async-start(f16[12,8,1792]{2,1,0:T(8,128)(2,1)} %multiply_convert_fusion), calls=%async_computation | async-start | bytes 688128 | tf_op jit(solution)/shard_map/all_to_all | solution.py:48
  36.7 0.7 shard_map.86.state
  37.4 15.2 %all-to-all-done = f16[12,8,1792]{2,1,0:T(8,128)(2,1)S(1)} async-done(((f16[12,8,1792]{2,1,0:T(8,128)(2,1)}), f16[12,8,1792]{2,1,0:T(8,128)(2,1)S(1)}, u32[]{:S(2)}, u32[]{:S(2)}) %all-to-all-start) | async-done | bytes 344096 | tf_op jit(solution)/shard_map/all_to_all | solution.py:48
  52.6 0.1 multiply_reduce_fusion.summed
  52.7 0.7 shard_map.87
  53.4 19.1 %all_to_all.15.received = f32[16,1,7296]{2,1,0:T(1,128)S(1)} all-to-all(f32[16,1,7296]{2,1,0:T(1,128)S(1)} %shard_map.87), channel_id=1, replica_groups=mesh['dp_0'=12,'dp_1'=2,'dp_2'=2,'tensor_0'=8,'tensor_1'=2] {'tensor_0',..., dimensions={0} | all-to-all | bytes 933888 | tf_op jit(solution)/shard_map/all_to_all | solution.py:48
  72.6 25.8 %all_to_all.16.squares = f32[48,1,128]{2,1,0:T(1,128)S(1)} all-to-all(f32[48,1,128]{2,1,0:T(1,128)S(1)} %broadcast_in_dim.2), channel_id=1, replica_groups=mesh['dp_0'=12,'dp_1'=2,'dp_2'=2,'tensor_0'=8,'tensor_1'=2] {'dp_0','dp_..., dimensions={0} | all-to-all | bytes 49152 | tf_op jit(solution)/shard_map/all_to_all | solution.py:48
  98.4 1.5 %shard_map.88 = (f32[8,1792]{1,0:T(8,128)}, f32[8,1792]{1,0:T(8,128)}, f32[8,1792]{1,0:T(8,128)}, bf16[8,1792]{1,0:T(8,128)(2,1)}) custom-call(s32[1,16]{1,0:T(1,128)} %owners.5, f32[48,1,128]{2,1,0:T(1,128)S(1)} %all_to_all.16.squares, f32[16,1,7296]{2,1,0:T(1,128)S(1)} %all_to_all.15.received, f32[8,1792]{1,0:T(8,128)S(1)} %multiply_reduce_fusion.summed, ...), custom_call_target="tpu_custom_call" | custom-call | tf_op jit(solution)/shard_map/pallas_call | solution.py:215
  (2 shorter events, 0.1 us)
Async XLA Ops:
  1.6 15.6 %collective-permute-start.1 = (bf16[12,8,1792]{2,1,0:T(8,128)(2,1)S(1)}, bf16[12,8,1792]{2,1,0:T(8,128)(2,1)S(1)}, u32[]{:S(2)}, u32[]{:S(2)}) collective-permute-start(bf16[12,8,1792]{2,1,0:T(8,128)(2,1)S(1)} %shard_map.85), channel_id=1, source_target_pairs={{0,16},{16,0},{1,17},{17,1},{2,18},{18,2},{3,19},{19,3},{4,20},{20... | collective-permute-start | bytes 1032200 | tf_op jit(solution)/shard_map/ppermute | solution.py:175
  15.3 4.0 %collective-permute-start = (bf16[12,8,1792]{2,1,0:T(8,128)(2,1)S(1)}, bf16[12,8,1792]{2,1,0:T(8,128)(2,1)S(1)}, u32[]{:S(2)}, u32[]{:S(2)}) collective-permute-start(bf16[12,8,1792]{2,1,0:T(8,128)(2,1)S(1)} %get-tuple-element.11), channel_id=1, source_target_pairs={{0,16},{16,0},{1,17},{17,1},{2,18},{18,2},{3,19},{19,3},{4,20},{20... | collective-permute-start | bytes 1032200 | tf_op jit(solution)/shard_map/ppermute | solution.py:183
  17.4 12.5 %collective-permute-start.2 = (f16[12,8,1792]{2,1,0:T(8,128)(2,1)S(1)}, f16[12,8,1792]{2,1,0:T(8,128)(2,1)S(1)}, u32[]{:S(2)}, u32[]{:S(2)}) collective-permute-start(f16[12,8,1792]{2,1,0:T(8,128)(2,1)S(1)} %multiply_convert_fusion.1), channel_id=1, source_target_pairs={{0,32},{32,0},{1,33},{33,1},{2,34},{34,2},{3,35},{35,3},{4,36},{36... | collective-permute-start | bytes 1032200 | tf_op jit(solution)/shard_map/ppermute | solution.py:197
  30.8 21.8 %all-to-all-start = ((f16[12,8,1792]{2,1,0:T(8,128)(2,1)}), f16[12,8,1792]{2,1,0:T(8,128)(2,1)S(1)}, u32[]{:S(2)}, u32[]{:S(2)}) async-start(f16[12,8,1792]{2,1,0:T(8,128)(2,1)} %multiply_convert_fusion), calls=%async_computation | async-start | bytes 688128 | tf_op jit(solution)/shard_map/all_to_all | solution.py:48
